TPU v7x, 256 devices: a whole 4x4x8 slice. The times are simulated.
256 devices in a mesh: dp: 32 (over y, x, core), tensor: 8 (over z).
Axes of the slice: x: 4, y: 4, z: 8, core: 2. Of those that a mesh axis runs over, the one named last changes fastest.
Arguments:
- frames: bfloat16 [8192, 4, 84, 84], P(('dp', 'tensor')), may hold values from 0 to 1
- counts: int32 [8, 32], replicated, may hold values from 1 to 32, 512 in all within a row
- slot_ids: int32 [32, 128], P('dp'), may hold values from 0 to 255, as said below
- reset_flags: int32 [32, 256], P('dp'), may hold values 0 or 1
- hidden_state: float32 [2048, 8192], P('tensor', 'dp'), may hold values from -1 to 1
- cell_state: float32 [2048, 8192], P('tensor', 'dp'), may hold values from -6 to 6
- conv_first: bfloat16 [16, 4, 3, 3], replicated, may hold values from -1.5 to 1.5
- conv_second: bfloat16 [32, 16, 3, 3], replicated, may hold values from -0.75 to 0.75
- conv_third: bfloat16 [32, 32, 3, 3], replicated, may hold values from -0.5 to 0.5
- res_first: bfloat16 [32, 32, 3, 3], replicated, may hold values from -0.5 to 0.5
- res_second: bfloat16 [32, 32, 3, 3], replicated, may hold values from -0.5 to 0.5
- projection: bfloat16 [256, 3872], replicated, may hold values from -0.125 to 0.125
- input_weight: bfloat16 [4, 2048, 256], P(None, 'tensor'), may hold values from -0.375 to 0.375
- recur_weight: bfloat16 [4, 2048, 2048], P(None, 'tensor'), may hold values from -0.125 to 0.125
- gate_bias: float32 [4, 2048], P(None, 'tensor'), may hold values from -3 to 3
- head_weight: bfloat16 [19, 2048], P(None, 'tensor'), may hold values from -0.125 to 0.125
Outputs:
- policy_out: float32 [19, 8192], P(None, ('dp', 'tensor'))
- hidden_after: float32 [2048, 8192], P('tensor', 'dp')
- cell_after: float32 [2048, 8192], P('tensor', 'dp')
Inputs may be any that keep to these rules, and one draw needn't show every extreme that they name: Arrival rows fill the first counts[t, a] slots of their device; each row of counts sums to 512. `slot_ids`: the entries of one dp index are distinct.
All inputs are finite; a program needn't handle non-finite values. No bound on the sum of `reset_flags` on one device may be relied on, other than what follows from the above.
Results may differ from a plain program's by a relative error of at most 0.008.
Values may be sent and summed in bfloat16 or wider, within the bound.
A program may use at most 128 MiB of HBM per device.

v0:
```python
import jax
import jax.numpy as jnp
from jax import lax
from jax.experimental import pallas as pl
from jax.experimental.pallas import tpu as pltpu
from jax.sharding import PartitionSpec as P

BF = jnp.bfloat16
F32 = jnp.float32
NEG = -3.0e38


def lanes(shape, dim):
    return lax.broadcasted_iota(jnp.int32, shape, dim)


def dot(a, b):
    return jnp.dot(a, b, preferred_element_type=F32)


def spread(w, width):
    pick = (lanes((width, 128), 1) % width == lanes((width, 128), 0)).astype(BF)
    return dot(w, pick)


def band_weights(out_ref, tiled, depth, spots, per_lane, columns, first):
    width = 128 // per_lane
    lane = lanes((depth, 128), 1) // width
    for ky in range(3):
        for p in range(spots):
            for col in range(columns):
                block = None
                for i in range(per_lane):
                    start = first(col, i)
                    if start is None:
                        continue
                    kx = p - start
                    if 0 <= kx <= 2:
                        row = (ky * 3 + kx) * depth
                        part = jnp.where(lane == i, tiled[row : row + depth], 0.0)
                        block = part if block is None else block + part
                if block is None:
                    block = jnp.zeros((depth, 128), F32)
                row = (ky * spots + p) * depth
                out_ref[row : row + depth, col * 128 : col * 128 + 128] = block.astype(BF)


def shifted(parts, pitch):
    lane = lanes(parts[0].shape, 1)
    rolled = [pltpu.roll(a, 128 - pitch, 1) for a in parts]
    return [
        jnp.where(lane < 128 - pitch, rolled[v], rolled[min(v + 1, len(parts) - 1)])
        for v in range(len(parts))
    ]


def encoder(
    frames, w1, w2, w3, r1, r2, pt, out,
    raw, flat, sel, k1, k2, k3, kr1, kr2, ptf, ptk, u, carry, p1, p2, p3, p3r, q1, sems,
):
    n = frames.shape[0]
    pairs = frames.shape[1]

    def fetch(q):
        return pltpu.make_async_copy(frames.at[:, q], raw.at[q], sems.at[q])

    def start(q, _):
        fetch(q).start()
        return 0

    lax.fori_loop(0, pairs, start, 0)

    x = lanes((128, 768), 0)
    col = lanes((128, 768), 1)
    p = col % 32
    hit = (x == (col // 128) * 16 - 11 + p) & (p < 18)
    for c in range(4):
        sel[c * 128 : c * 128 + 128] = jnp.where(hit & (col // 32 % 4 == c), 1.0, 0.0).astype(BF)
    t1 = spread(w1[...], 16)
    t1 = jnp.concatenate([t1, t1], axis=1)
    kx = lanes((32, 256), 0) - 2 * (lanes((32, 256), 1) // 16 % 8) - lanes((32, 256), 1) // 128
    for ky in range(3):
        for c in range(4):
            block = jnp.zeros((32, 256), F32)
            for k in range(3):
                row = (ky * 3 + k) * 4 + c
                block = jnp.where(kx == k, t1[row : row + 1], block)
            row = ky * 128 + c * 32
            k1[row : row + 32] = block.astype(BF)
    both = lambda col, i: 2 * i + col
    band_weights(k2, spread(w2[...], 32), 16, 16, 4, 2, both)
    band_weights(k3, spread(w3[...], 32), 32, 12, 4, 2, both)
    same = lambda col, i: None if col * 4 + i > 10 else col * 4 + i - 1
    band_weights(kr1, spread(r1[...], 32), 32, 12, 4, 3, same)
    band_weights(kr2, spread(r2[...], 32), 32, 12, 4, 3, same)

    def widen(i, _):
        rows = pl.ds(i * 352, 352)
        block = pt[rows, :].astype(F32)
        ptf[0, rows, :] = block[:, :128]
        ptf[1, rows, :] = block[:, 128:]
        return 0

    lax.fori_loop(0, 11, widen, 0)

    def reorder(y, _):
        for px in range(11):
            rows = pl.ds(y * 384 + px * 32, 32)
            for h in range(2):
                ptk[rows, h * 128 : h * 128 + 128] = ptf[
                    h, pl.ds(y * 11 + px, 32, stride=121), :
                ].astype(BF)
        ptk[pl.ds(y * 384 + 352, 32), :] = jnp.zeros((32, 256), BF)
        return 0

    lax.fori_loop(0, 11, reorder, 0)

    u[0] = jnp.zeros((n, 768), BF)
    u[2 * pairs + 1] = jnp.zeros((n, 768), BF)
    u[2 * pairs + 2] = jnp.zeros((n, 768), BF)
    p1[0] = jnp.zeros((n, 896), BF)
    p1[43] = jnp.zeros((n, 896), BF)
    p1[44] = jnp.zeros((n, 896), BF)
    p2[0] = jnp.zeros((n, 896), BF)
    p2[22] = jnp.zeros((n, 896), BF)
    p2[23] = jnp.zeros((n, 896), BF)
    for ref in (p3r, q1):
        ref[0] = jnp.zeros((n, 384), BF)
        ref[12] = jnp.zeros((n, 384), BF)
    flat[...] = jnp.zeros_like(flat)

    def windows(q, _):
        fetch(q).wait()
        flat[:, 0:84] = raw[q].astype(F32).reshape(n * 8, 84)
        rows = []
        for y in range(2):
            rows.append(
                jnp.concatenate(
                    [flat[pl.ds(y * 4 + c, n, stride=8), :].astype(BF) for c in range(4)], axis=1
                )
            )
        cut = dot(jnp.concatenate(rows, axis=0), sel[...]).astype(BF)
        u[2 * q + 1] = cut[:n]
        u[2 * q + 2] = cut[n:]
        return 0

    lax.fori_loop(0, pairs, windows, 0)

    def conv_row(src, y, count, step, width, weights):
        taps = [src[y + ky] for ky in range(3)]
        lhs = [
            jnp.concatenate([t[:, v * step : v * step + width] for t in taps], axis=1)
            for v in range(count)
        ]
        return lhs

    def pool_stage(src, dst, count, step, width, weights, per, pitch, offset, limit, last):
        carry[0 : count * n] = dot(
            jnp.concatenate(conv_row(src, 0, count, step, width, weights), axis=0), weights[...]
        )
        lane = lanes((n, 128), 1) // pitch

        def body(y, _):
            lhs = conv_row(src, 2 * y + 1, count, step, width, weights) + conv_row(
                src, 2 * y + 2, count, step, width, weights
            )
            acc = dot(jnp.concatenate(lhs, axis=0), weights[...])
            later = acc[count * n :] * jnp.where(y < last, 1.0, 0.0)
            top = jnp.maximum(jnp.maximum(carry[0 : count * n], acc[: count * n]), later)
            carry[0 : count * n] = later
            top = jnp.maximum(top, 0.0)
            even = [top[v * n : v * n + n, :128] for v in range(count)]
            odd = [top[v * n : v * n + n, 128:] for v in range(count)]
            spots = [lane + (v * per - offset) for v in range(count)]
            even[-1] = jnp.where(spots[-1] < limit, even[-1], 0.0)
            nxt = shifted(even, pitch)
            for v in range(count):
                best = jnp.maximum(jnp.maximum(even[v], odd[v]), nxt[v])
                if v == 0 or v == count - 1:
                    best = jnp.where((spots[v] >= 0) & (spots[v] < limit), best, 0.0)
                dst[y + 1, :, v * 128 : v * 128 + 128] = best.astype(BF)
            dst[y + 1, :, count * 128 : count * 128 + 128] = jnp.zeros((n, 128), BF)
            return 0

        lax.fori_loop(0, last + 1, body, 0)

    pool_stage(u, p1, 6, 128, 128, k1, 8, 16, 5, 42, 41)
    pool_stage(p1, p2, 6, 128, 256, k2, 4, 32, 2, 21, 20)

    lane = lanes((n, 128), 1) // 32
    carry[0 : 3 * n] = jnp.full((3 * n, 256), NEG, F32)

    def third(y, _):
        lhs = conv_row(p2, 2 * y, 3, 256, 384, k3) + conv_row(p2, 2 * y + 1, 3, 256, 384, k3)
        acc = dot(jnp.concatenate(lhs, axis=0), k3[...])
        later = jnp.where(y < 10, acc[3 * n :], NEG)
        top = jnp.maximum(jnp.maximum(carry[0 : 3 * n], acc[: 3 * n]), later)
        carry[0 : 3 * n] = later
        even = [top[v * n : v * n + n, :128] for v in range(3)]
        odd = [top[v * n : v * n + n, 128:] for v in range(3)]
        even[0] = jnp.where(lane == 0, NEG, even[0])
        even[2] = jnp.where(lane == 3, NEG, even[2])
        nxt = shifted(even, 32)
        for v in range(3):
            best = jnp.maximum(jnp.maximum(even[v], odd[v]), nxt[v])
            if v == 2:
                best = jnp.where(lane == 3, 0.0, best)
            p3[y, :, v * 128 : v * 128 + 128] = best.astype(BF)
            p3r[y + 1, :, v * 128 : v * 128 + 128] = jnp.maximum(best, 0.0).astype(BF)
        return 0

    lax.fori_loop(0, 11, third, 0)

    def full_rows(src):
        return jnp.concatenate(
            [jnp.concatenate([src[y + ky] for ky in range(3)], axis=1) for y in range(11)], axis=0
        )

    q1[1:12] = jnp.maximum(dot(full_rows(p3r), kr1[...]), 0.0).astype(BF).reshape(11, n, 384)
    final = dot(full_rows(q1), kr2[...]) + p3[...].reshape(11 * n, 384).astype(F32)
    final = jnp.maximum(final, 0.0).astype(BF)
    line = jnp.concatenate([final[y * n : y * n + n] for y in range(11)], axis=1)
    out[...] = jnp.maximum(dot(line, ptk[...]), 0.0).astype(BF)


def encode(frames, conv_first, conv_second, conv_third, res_first, res_second, projection):
    n = frames.shape[0]
    tiles = frames.transpose(0, 2, 1, 3).reshape(n, 42, 8, 84)
    flatw = lambda w: w.transpose(2, 3, 1, 0).reshape(-1, w.shape[0])
    vm = lambda *s: pltpu.VMEM(s, BF)
    vmf = lambda *s: pltpu.VMEM(s, F32)
    return pl.pallas_call(
        encoder,
        out_shape=jax.ShapeDtypeStruct((n, 256), BF),
        in_specs=[pl.BlockSpec(memory_space=pl.ANY)] + [pl.BlockSpec(memory_space=pltpu.VMEM)] * 6,
        out_specs=pl.BlockSpec(memory_space=pltpu.VMEM),
        scratch_shapes=[
            vm(42, n, 8, 84), vmf(n * 8, 128), vm(512, 768), vm(384, 256), vm(768, 256),
            vm(1152, 256), vm(1152, 384), vm(1152, 384), vmf(2, 3872, 128), vm(4224, 256),
            vm(87, n, 768), vmf(6 * n, 256), vm(45, n, 896), vm(24, n, 896),
            vm(11, n, 384), vm(13, n, 384), vm(13, n, 384), pltpu.SemaphoreType.DMA((42,)),
        ],
        compiler_params=pltpu.CompilerParams(vmem_limit_bytes=60 * 1024 * 1024),
    )(tiles, flatw(conv_first), flatw(conv_second), flatw(conv_third), flatw(res_first), flatw(res_second), projection.T)


def joined_along(blocks, dim):
    lengths = list(blocks.shape[1:])
    lengths[dim] *= blocks.shape[0]
    return jnp.moveaxis(blocks, 0, dim).reshape(lengths)


def gather_together(arrays, axis, dims):
    ravelled = jnp.concatenate([a.reshape(-1) for a in arrays])
    lines, at, outs = (lax.all_gather(ravelled, axis), 0, [])
    for a, dim in zip(arrays, dims):
        blocks = lines[:, at : at + a.size].reshape(-1, *a.shape)
        outs.append(joined_along(blocks, dim))
        at += a.size
    return tuple(outs)


def copy_for_each(shard, axis):
    copies = jnp.broadcast_to(shard, (lax.axis_size(axis), *shard.shape))
    return lax.all_to_all(copies, axis, split_axis=0, concat_axis=0, tiled=True)


def over_copies(shard, axis):
    everything = copy_for_each(shard, axis)
    return jnp.sum(everything, axis=0)


def body(
    frames,
    counts,
    slot_ids,
    reset_flags,
    hidden_state,
    cell_state,
    conv_first,
    conv_second,
    conv_third,
    res_first,
    res_second,
    projection,
    input_weight,
    recur_weight,
    gate_bias,
    head_weight,
):
    dp_count = lax.axis_size("dp")
    tensor_count = lax.axis_size("tensor")
    dp_index = lax.axis_index("dp")
    tensor_index = lax.axis_index("tensor")
    capacity = frames.shape[0]
    pair_depth = capacity // dp_count
    per_device = slot_ids.shape[1] // tensor_count
    tallies = lax.dynamic_index_in_dim(counts, tensor_index, 0, keepdims=False)
    starts = jnp.cumsum(tallies, dtype=jnp.int32) - tallies
    range_ends = starts + tallies
    own_start = lax.dynamic_index_in_dim(starts, dp_index, 0, keepdims=False)
    own_count = lax.dynamic_index_in_dim(tallies, dp_index, 0, keepdims=False)
    peer_index = jnp.arange(dp_count, dtype=jnp.int32)
    levels = jnp.arange(pair_depth, dtype=jnp.int32)
    send_rows = ((peer_index[:, None] - own_start) % dp_count + levels[None, :] * dp_count).reshape(
        -1
    )
    send_live = send_rows < own_count
    send_safe = jnp.minimum(send_rows, capacity - 1)
    balanced_ranks = jnp.arange(per_device, dtype=jnp.int32) * dp_count + dp_index
    source = jnp.sum((range_ends[:, None] <= balanced_ranks[None, :]).astype(jnp.int32), axis=0)
    offset = balanced_ranks - jnp.take(starts, source)
    take_slots = source * pair_depth + offset // dp_count
    own = encode(
        frames, conv_first, conv_second, conv_third, res_first, res_second, projection
    )
    outgoing = jnp.where(
        send_live[:, None], jnp.take(own, send_safe, axis=0), jnp.zeros((), jnp.bfloat16)
    )
    incoming = lax.all_to_all(outgoing, "dp", split_axis=0, concat_axis=0, tiled=True)
    features = jnp.take(incoming, take_slots, axis=0).T
    chosen = slot_ids[0]
    keep_state = (1 - jnp.take(reset_flags[0], chosen)).astype(jnp.float32)
    prev_hidden = jnp.take(hidden_state, chosen, axis=1) * keep_state[None, :]
    prev_cell = jnp.take(cell_state, chosen, axis=1) * keep_state[None, :]
    all_features, all_hidden = gather_together(
        (features, prev_hidden.astype(jnp.bfloat16)), "tensor", (1, 0)
    )
    hidden_share = hidden_state.shape[0]
    gate_sums = jnp.dot(
        input_weight.reshape(4 * hidden_share, -1), all_features, preferred_element_type=jnp.float32
    )
    gate_sums = gate_sums + jnp.dot(
        recur_weight.reshape(4 * hidden_share, -1), all_hidden, preferred_element_type=jnp.float32
    )
    gate_sums = (gate_sums + gate_bias.reshape(4 * hidden_share, 1)).reshape(4, hidden_share, -1)
    next_cell = jax.nn.sigmoid(gate_sums[1]) * prev_cell + jax.nn.sigmoid(gate_sums[0]) * jnp.tanh(
        gate_sums[2]
    )
    next_hidden = jax.nn.sigmoid(gate_sums[3]) * jnp.tanh(next_cell)
    hidden_after = hidden_state.at[:, chosen].set(next_hidden)
    cell_after = cell_state.at[:, chosen].set(next_cell)
    partial_heads = jnp.dot(
        head_weight, next_hidden.astype(jnp.bfloat16), preferred_element_type=jnp.float32
    )
    totals = over_copies(partial_heads, "tensor")
    own_heads = lax.dynamic_slice_in_dim(totals, tensor_index * per_device, per_device, 1)
    back_rows = (dp_index - starts[:, None]) % dp_count + levels[None, :] * dp_count
    back_live = (back_rows < tallies[:, None]).reshape(-1)
    back_place = jnp.minimum((starts[:, None] + back_rows) // dp_count, per_device - 1).reshape(-1)
    outgoing_heads = jnp.where(back_live[None, :], jnp.take(own_heads, back_place, axis=1), 0.0)
    returned = lax.all_to_all(outgoing_heads, "dp", split_axis=1, concat_axis=1, tiled=True)
    arrivals = jnp.arange(capacity, dtype=jnp.int32)
    home_slots = (own_start + arrivals) % dp_count * pair_depth + arrivals // dp_count
    policy_out = jnp.where(
        (arrivals < own_count)[None, :], jnp.take(returned, home_slots, axis=1), 0.0
    )
    return (policy_out, hidden_after, cell_after)


def solution(mesh):
    return jax.shard_map(
        body,
        mesh=mesh,
        in_specs=(
            P(("dp", "tensor"), None, None, None),
            P(),
            P("dp", None),
            P("dp", None),
            P("tensor", "dp"),
            P("tensor", "dp"),
            P(),
            P(),
            P(),
            P(),
            P(),
            P(),
            P(None, "tensor", None),
            P(None, "tensor", None),
            P(None, "tensor"),
            P(None, "tensor"),
        ),
        out_specs=(P(None, ("dp", "tensor")), P("tensor", "dp"), P("tensor", "dp")),
        check_vma=False,
    )
```

profile of v0, /device:TPU:1, one launch (start us, length us, event | category | flops | bytes accessed | tf_op | source)
XLA Modules:
  0.0 140.8 jit_solution(12173232015264410867)
XLA Ops:
  0.7 0.8 fusion.58
  1.4 1.3 reshape.643.w1
  2.9 0.1 fusion.32
  3.0 0.7 compare_and_fusion.3
  3.8 0.6 dynamic_slice.16
  4.3 0.7 fusion.31
  5.0 1.4 dynamic_slice.14
  6.4 1.3 compare_and_fusion.1
  7.7 1.6 %copy.99 = bf16[3,3,32,32]{3,2,1,0:T(8,128)(2,1)} copy(bf16[3,3,32,32]{2,3,1,0:T(8,128)(2,1)} %bitcast.125) | data formatting | bytes 36864 | tf_op jit(solution)/shard_map/transpose | solution.py:229
  9.3 1.6 %copy.100 = bf16[3,3,32,32]{3,2,1,0:T(8,128)(2,1)} copy(bf16[3,3,32,32]{2,3,1,0:T(8,128)(2,1)} %bitcast.126) | data formatting | bytes 36864 | tf_op jit(solution)/shard_map/transpose | solution.py:229
  10.9 1.6 %copy.101 = bf16[3,3,32,32]{3,2,1,0:T(8,128)(2,1)} copy(bf16[3,3,32,32]{2,3,1,0:T(8,128)(2,1)} %bitcast.127) | data formatting | bytes 36864 | tf_op jit(solution)/shard_map/transpose | solution.py:229
  12.5 43.6 %shard_map.175 = bf16[32,256]{1,0:T(8,128)(2,1)} custom-call(bf16[32,42,8,84]{3,2,1,0:T(8,128)(2,1)} %bitcast.115, bf16[36,16]{1,0:T(8,128)(2,1)} %reshape.643.w1, bf16[144,32]{1,0:T(8,128)(2,1)} %bitcast.128, bf16[288,32]{1,0:T(8,128)(2,1)} %bitcast.120, bf16[288,32]{1,0:T(8,128)(2,1)} %bitcast.121, bf16[288,32]{1,0:T(8,128)(2,1)} %bitcast.122, ...), custom_call_target="tpu_custom_call" | custom-call | tf_op jit(solution)/shard_map/pallas_call | solution.py:232
  56.1 1.3 gather_fusion.1
  57.5 0.5 broadcast.927
  58.0 0.7 reduce.9
  58.7 0.6 reshape.750
  59.3 8.6 %all-to-all-start = ((bf16[32,2,128]{2,1,0:T(2,128)(2,1)}), bf16[32,2,128]{2,1,0:T(2,128)(2,1)S(1)}, u32[]{:S(2)}, u32[]{:S(2)}) async-start(bf16[32,2,128]{2,1,0:T(2,128)(2,1)} %reshape.750), calls=%async_computation | async-start | bytes 32768 | tf_op jit(solution)/shard_map/all_to_all | solution.py:320
  68.0 0.7 compare_bitcast_fusion
  68.7 0.2 convert_reduce_fusion
  68.9 0.7 gather_fusion
  69.6 1.3 gather_fusion.3
  71.1 0.8 gather_fusion.6
  72.2 0.8 gather_fusion.7
  73.0 0.7 fusion.39
  73.7 1.1 all-to-all-done
  74.8 0.6 gather_fusion.2
  75.7 23.1 %all-gather = bf16[294912]{0:T(1024)(128)(2,1)S(1)} all-gather(bf16[36864]{0:T(1024)(128)(2,1)S(1)} %pad_maximum_fusion), channel_id=2, replica_groups=mesh['dp'=32,'tensor'=8] {'tensor'}, dimensions={0}, use_global_device_ids=true | all-gather | bytes 663552 | tf_op jit(solution)/shard_map/all_gather | solution.py:255
  98.8 0.3 reshape.734
  99.1 0.2 reshape_reshape.3
  99.4 0.4 reshape.650
  99.8 0.2 copy.106
  100.0 0.3 fusion.61
  100.3 3.7 %fusion.1 = f32[1024,128]{0,1:T(8,128)S(1)} fusion(f32[128,1024]{1,0:T(8,128)S(1)} %fusion.61, bf16[2048,128]{1,0:T(8,128)(2,1)S(1)} %reshape_reshape.3, bf16[1024,2048]{1,0:T(8,128)(2,1)} %bitcast.114, f32[1024]{0:T(1024)S(1)} %bitcast.129), kind=kOutput, calls=%fused_computation.12 | convolution fusion | flops 537133056 | bytes 5771264 | tf_op jit(solution)/shard_map/dot_general | solution.py:333
  104.1 0.2 convolution_bitcast_fusion
  104.3 0.7 broadcast_in_dim.123
  105.0 5.1 %all-to-all-start.1 = ((f32[8,19,128]{2,1,0:T(8,128)}), f32[8,19,128]{2,1,0:T(8,128)S(1)}, u32[]{:S(2)}, u32[]{:S(2)}) async-start(f32[8,19,128]{2,1,0:T(8,128)} %broadcast_in_dim.123), calls=%async_computation.1 | async-start | bytes 196608 | tf_op jit(solution)/shard_map/all_to_all | solution.py:265
  110.1 7.6 %all-to-all-done.1 = f32[8,19,128]{2,1,0:T(8,128)S(1)} async-done(((f32[8,19,128]{2,1,0:T(8,128)}), f32[8,19,128]{2,1,0:T(8,128)S(1)}, u32[]{:S(2)}, u32[]{:S(2)}) %all-to-all-start.1) | async-done | bytes 77856 | tf_op jit(solution)/shard_map/all_to_all | solution.py:265
  117.8 0.6 gather_fusion.4
  118.4 0.7 fusion.33
  119.1 13.4 %all-to-all-start.2 = ((f32[19,32,1]{0,2,1:T(1,128)}), f32[19,32,1]{0,2,1:T(1,128)S(1)}, u32[]{:S(2)}, u32[]{:S(2)}) async-start(f32[19,32,1]{0,2,1:T(1,128)} %bitcast.40), calls=%async_computation.2 | async-start | bytes 32768 | tf_op jit(solution)/shard_map/all_to_all | solution.py:352
  132.5 1.3 compare_and_fusion.4
  133.7 1.2 scatter_custom_fusion
  134.9 1.1 scatter_custom_fusion.1
  136.1 0.8 copy.116
  136.9 0.8 copy.115
  137.8 1.7 %all-to-all-done.2 = f32[19,32,1]{0,2,1:T(1,128)S(1)} async-done(((f32[19,32,1]{0,2,1:T(1,128)}), f32[19,32,1]{0,2,1:T(1,128)S(1)}, u32[]{:S(2)}, u32[]{:S(2)}) %all-to-all-start.2) | async-done | bytes 2464 | tf_op jit(solution)/shard_map/all_to_all | solution.py:352
  139.4 0.6 gather_fusion.5
  140.1 0.7 copy.114
  (50 shorter events, 1.6 us)
Async XLA Ops:
  0.6 99.3 %copy-start = (bf16[4,256,256]{2,1,0:T(8,128)(2,1)S(1)}, bf16[4,256,256]{2,1,0:T(8,128)(2,1)}, u32[]{:S(2)}) copy-start(bf16[4,256,256]{2,1,0:T(8,128)(2,1)} %param.30) | copy-start | bytes 1572868
  0.6 67.3 %copy-start.6 = (s32[1,128]{1,0:T(1,128)S(1)}, s32[1,128]{1,0:T(1,128)}, u32[]{:S(2)}) copy-start(s32[1,128]{1,0:T(1,128)} %param.20) | copy-start | bytes 1540
  0.7 69.0 %copy-start.1 = (s32[1,256]{1,0:T(1,128)S(1)}, s32[1,256]{1,0:T(1,128)}, u32[]{:S(2)}) copy-start(s32[1,256]{1,0:T(1,128)} %param.21) | copy-start | bytes 3076
  0.7 70.2 %copy-start.2 = (f32[256,256]{1,0:T(8,128)S(1)}, f32[256,256]{1,0:T(8,128)}, u32[]{:S(2)}) copy-start(f32[256,256]{1,0:T(8,128)} %param.22) | copy-start | bytes 786436
  10.9 61.1 %copy-start.4 = (f32[4,256]{1,0:T(4,128)S(1)}, f32[4,256]{1,0:T(4,128)}, u32[]{:S(2)}) copy-start(f32[4,256]{1,0:T(4,128)} %param.32) | copy-start | bytes 12292
  12.5 59.6 %copy-start.3 = (f32[256,256]{1,0:T(8,128)S(1)}, f32[256,256]{1,0:T(8,128)}, u32[]{:S(2)}) copy-start(f32[256,256]{1,0:T(8,128)} %param.23) | copy-start | bytes 786436
  59.3 15.5 %all-to-all-start = ((bf16[32,2,128]{2,1,0:T(2,128)(2,1)}), bf16[32,2,128]{2,1,0:T(2,128)(2,1)S(1)}, u32[]{:S(2)}, u32[]{:S(2)}) async-start(bf16[32,2,128]{2,1,0:T(2,128)(2,1)} %reshape.750), calls=%async_computation | async-start | bytes 32768 | tf_op jit(solution)/shard_map/all_to_all | solution.py:320
  99.8 4.4 %copy-start.5 = (bf16[19,256]{1,0:T(8,128)(2,1)S(1)}, bf16[19,256]{1,0:T(8,128)(2,1)}, u32[]{:S(2)}) copy-start(bf16[19,256]{1,0:T(8,128)(2,1)} %param.33) | copy-start | bytes 29188
  105.0 12.7 %all-to-all-start.1 = ((f32[8,19,128]{2,1,0:T(8,128)}), f32[8,19,128]{2,1,0:T(8,128)S(1)}, u32[]{:S(2)}, u32[]{:S(2)}) async-start(f32[8,19,128]{2,1,0:T(8,128)} %broadcast_in_dim.123), calls=%async_computation.1 | async-start | bytes 196608 | tf_op jit(solution)/shard_map/all_to_all | solution.py:265
  119.1 20.3 %all-to-all-start.2 = ((f32[19,32,1]{0,2,1:T(1,128)}), f32[19,32,1]{0,2,1:T(1,128)S(1)}, u32[]{:S(2)}, u32[]{:S(2)}) async-start(f32[19,32,1]{0,2,1:T(1,128)} %bitcast.40), calls=%async_computation.2 | async-start | bytes 32768 | tf_op jit(solution)/shard_map/all_to_all | solution.py:352
where the time goes:
time: 141 us
  Pallas kernels  43.6 us (31%)
  starting transfers between devices  27.1 us (19%)
  blocking collectives  23.1 us (16%)
  local copies, waits for them, and re-layouts  22.6 us (16%)
  waiting for transfers between devices  10.4 us (7%)
  other arithmetic  8.79 us (6%)
  matrix products  4.21 us (3%)
    pallas_call x1, Pallas kernels, encode(): pl.pallas_call(encoder, out_shape=jax.ShapeDtypeStruct((n, 256), BF), in_...  43.6 us
    all_gather x1, blocking collectives, gather_together(): lines, at, outs = (lax.all_gather(ravelled, axis), 0, [])  23.1 us
    all_to_all x1, starting transfers between devices, body(): lax.all_to_all(outgoing_heads, 'dp', split_axis=1, concat_axis=1, tiled=T...  13.4 us
    all_to_all x1, starting transfers between devices, body(): lax.all_to_all(outgoing, 'dp', split_axis=0, concat_axis=0, tiled=True)  8.6 us
    all_to_all x1, waiting for transfers between devices, copy_for_each(): return lax.all_to_all(copies, axis, split_axis=0, concat_axis=0, tiled=True)  7.56 us
    all_to_all x1, starting transfers between devices, copy_for_each(): return lax.all_to_all(copies, axis, split_axis=0, concat_axis=0, tiled=True)  5.12 us
    transpose x3, local copies, waits for them, and re-layouts, encode(): flatw = lambda w: w.transpose(2, 3, 1, 0).reshape(-1, w.shape[0])  4.84 us
    dot_general x1, matrix products, body(): jnp.dot(recur_weight.reshape(4 * hidden_share, -1), all_hidden, preferred...  3.71 us
  transfers between devices with their start and end apart: 3, of which 3 were waited for; matrix products, arithmetic and copies ran while one was open for 8% of the time, Pallas kernels for 0%

commit v1 on v0

--- a/solution.py
+++ b/solution.py
@@ -54,21 +54,159 @@
     ]
 
 
+def count_tables(counts, me_t, me_d, cap, per):
+    nd = counts.shape[1]
+    own = counts[pl.ds(me_t, 1), :].astype(F32)
+    a_row = lanes((nd, nd), 1)
+    a_col = lanes((nd, nd), 0)
+    wide = jnp.broadcast_to(own, (nd, nd))
+    start_col = jnp.sum(jnp.where(a_row < a_col, wide, 0.0), axis=1, keepdims=True)
+    count_col = jnp.sum(jnp.where(a_row == a_col, wide, 0.0), axis=1, keepdims=True)
+    start_row = jnp.sum(
+        jnp.where(a_col < a_row, jnp.broadcast_to(count_col, (nd, nd)), 0.0), axis=0, keepdims=True
+    )
+    mine = lanes((1, nd), 1) == me_d
+    start = jnp.sum(jnp.where(mine, start_row, 0.0), axis=1, keepdims=True).astype(jnp.int32)
+    count = jnp.sum(jnp.where(mine, own, 0.0), axis=1, keepdims=True).astype(jnp.int32)
+    b, j = lanes((nd, cap), 0), lanes((nd, cap), 1)
+    send = (jnp.bitwise_and(b - start - j, nd - 1) == 0) & (j < count)
+    rank = (lanes((per, nd), 0) * nd + me_d).astype(F32)
+    take = (start_row <= rank) & (rank < start_row + own)
+    rank = (lanes((nd, per), 1) * nd + me_d).astype(F32)
+    give = (start_col <= rank) & (rank < start_col + count_col)
+    j, b = lanes((cap, nd), 0), lanes((cap, nd), 1)
+    home = (jnp.bitwise_and(b - start - j, nd - 1) == 0) & (j < count)
+    as_f32 = lambda m: jnp.where(m, 1.0, 0.0)
+    return as_f32(send), as_f32(take), as_f32(give), as_f32(home)
+
+
+def dot_nt(a, b):
+    return lax.dot_general(a, b, (((1,), (1,)), ((), ())), preferred_element_type=F32)
+
+
+def exact(a, b):
+    return jnp.dot(a, b, precision=lax.Precision.HIGHEST, preferred_element_type=F32)
+
+
+class Ring:
+    def __init__(self, axis, other):
+        self.axis, self.size, self.me = axis, lax.axis_size(axis), lax.axis_index(axis)
+        self.other = lax.axis_index(other)
+
+    def place(self, peer):
+        return (peer, self.other) if self.axis == "dp" else (self.other, peer)
+
+    def each(self, act):
+        def step(k, _):
+            act(k, lax.rem(self.me + k, self.size))
+            return 0
+
+        lax.fori_loop(1, self.size, step, 0)
+
+    def copy(self, k, peer, src, dst, sems):
+        return pltpu.make_async_remote_copy(
+            src_ref=src, dst_ref=dst, send_sem=sems.at[0, k], recv_sem=sems.at[1, k],
+            device_id=self.place(peer), device_id_type=pl.DeviceIdType.MESH,
+        )
+
+
+def greet(rings):
+    barrier = pltpu.get_barrier_semaphore()
+    for ring in rings:
+        ring.each(
+            lambda k, peer, ring=ring: pl.semaphore_signal(
+                barrier, inc=1, device_id=ring.place(peer), device_id_type=pl.DeviceIdType.MESH
+            )
+        )
+    pl.semaphore_wait(barrier, sum(ring.size - 1 for ring in rings))
+
+
+def send_hidden(ring, ids, reset, hid, hall, sems):
+    slots, rows = hid.shape[1], ids.shape[1]
+    keep = (1 - reset[...]).astype(F32)
+    pick = jnp.where(lanes((slots, rows), 0) == ids[...], 1.0, 0.0)
+    hall[ring.me] = dot((hid[...] * keep).astype(BF), pick.astype(BF)).astype(BF)
+    copy = lambda k, peer: ring.copy(k, peer, hall.at[ring.me], hall.at[ring.me], sems)
+    ring.each(lambda k, peer: copy(k, peer).start())
+    return copy
+
+
+def core(
+    feat, dp, tp, hidden_copy, waits,
+    counts, ids, reset, bias, head, hid, cell, win, wrec,
+    out, hout, cout,
+    hall, orow, inrow, fall, hp, hin, brow, rrow, gates, sem_f, sem_g, sem_h, sem_b,
+):
+    cap, per = feat.shape[0], fall.shape[1]
+    share, slots = hid.shape
+    rows = ids.shape[1]
+    send, take, give, home = count_tables(counts, tp.me, dp.me, cap, per)
+
+    spread_rows = dot(send.astype(BF), feat)
+    for b in range(dp.size):
+        orow[b] = spread_rows[b : b + 1]
+    inrow[dp.me] = orow[dp.me]
+    row_copy = lambda k, peer: dp.copy(k, peer, orow.at[peer], inrow.at[dp.me], sem_f)
+    dp.each(lambda k, peer: row_copy(k, peer).start())
+
+    waits()
+    keep = (1 - reset[...]).astype(F32)
+    pick = jnp.where(lanes((slots, rows), 0) == ids[...], 1.0, 0.0)
+    tp.each(lambda k, peer: hidden_copy(k, peer).wait())
+    everyone = hall[...].reshape(tp.size * share, rows)
+    recurrent = []
+    for q in range(4):
+        tall = jnp.transpose(jnp.broadcast_to(bias[q : q + 1, :], (8, share)))[:, 0:1]
+        gates[q * share : (q + 1) * share] = dot(wrec[q * share : (q + 1) * share], everyone) + tall
+    prev_cell = exact(cell[...] * keep, pick)
+
+    dp.each(lambda k, peer: row_copy(k, peer).wait())
+    gathered = jnp.concatenate([inrow[a] for a in range(dp.size)], axis=0)
+    fall[tp.me] = dot(take.astype(BF), gathered.astype(BF)).astype(BF)
+    feat_copy = lambda k, peer: tp.copy(k, peer, fall.at[tp.me], fall.at[tp.me], sem_g)
+    tp.each(lambda k, peer: feat_copy(k, peer).start())
+    tp.each(lambda k, peer: feat_copy(k, peer).wait())
+
+    features = fall[...].reshape(rows, fall.shape[2])
+    sums = gates[...] + dot_nt(win[...], features)
+    gate = [sums[q * share : (q + 1) * share] for q in range(4)]
+    next_cell = jax.nn.sigmoid(gate[1]) * prev_cell + jax.nn.sigmoid(gate[0]) * jnp.tanh(gate[2])
+    next_hidden = jax.nn.sigmoid(gate[3]) * jnp.tanh(next_cell)
+    partial = jnp.transpose(dot(head[...], next_hidden.astype(BF)))
+    width = partial.shape[1]
+    for t in range(tp.size):
+        hp[t, :, 0:width] = partial[t * per : (t + 1) * per]
+    hin[tp.me] = hp[tp.me]
+    sum_copy = lambda k, peer: tp.copy(k, peer, hp.at[peer], hin.at[tp.me], sem_h)
+    tp.each(lambda k, peer: sum_copy(k, peer).start())
+
+    square = lanes((rows, rows), 0) == lanes((rows, rows), 1)
+    column = jnp.sum(jnp.where(square, ids[...], 0).astype(F32), axis=1, keepdims=True)
+    lay = jnp.where(lanes((rows, slots), 1).astype(F32) == column, 1.0, 0.0)
+    chosen = jnp.sum(lay, axis=0, keepdims=True) > 0.0
+    hout[...] = jnp.where(chosen, exact(next_hidden, lay), hid[...])
+    cout[...] = jnp.where(chosen, exact(next_cell, lay), cell[...])
+
+    tp.each(lambda k, peer: sum_copy(k, peer).wait())
+    total = hin[0]
+    for t in range(1, tp.size):
+        total = total + hin[t]
+    back = exact(give, total)
+    for a in range(dp.size):
+        brow[a] = back[a : a + 1]
+    rrow[dp.me] = brow[dp.me]
+    back_copy = lambda k, peer: dp.copy(k, peer, brow.at[peer], rrow.at[dp.me], sem_b)
+    dp.each(lambda k, peer: back_copy(k, peer).start())
+    dp.each(lambda k, peer: back_copy(k, peer).wait())
+    heads = exact(home, jnp.concatenate([rrow[a] for a in range(dp.size)], axis=0))
+    out[...] = jnp.transpose(heads)[0 : out.shape[0], :]
+
+
 def encoder(
-    frames, w1, w2, w3, r1, r2, pt, out,
-    raw, flat, sel, k1, k2, k3, kr1, kr2, ptf, ptk, u, carry, p1, p2, p3, p3r, q1, sems,
+    fetch, fetch_dense, after_weights, w1, w2, w3, r1, r2, pt,
+    raw, flat, sel, k1, k2, k3, kr1, kr2, ptf, ptk, u, carry, p1, p2, p3, p3r, q1,
 ):
-    n = frames.shape[0]
-    pairs = frames.shape[1]
-
-    def fetch(q):
-        return pltpu.make_async_copy(frames.at[:, q], raw.at[q], sems.at[q])
-
-    def start(q, _):
-        fetch(q).start()
-        return 0
-
-    lax.fori_loop(0, pairs, start, 0)
+    pairs, n = raw.shape[0:2]
 
     x = lanes((128, 768), 0)
     col = lanes((128, 768), 1)
@@ -94,6 +232,9 @@
     band_weights(kr1, spread(r1[...], 32), 32, 12, 4, 3, same)
     band_weights(kr2, spread(r2[...], 32), 32, 12, 4, 3, same)
 
+    after_weights()
+    fetch_dense()
+
     def widen(i, _):
         rows = pl.ds(i * 352, 352)
         block = pt[rows, :].astype(F32)
@@ -220,142 +361,103 @@
     final = dot(full_rows(q1), kr2[...]) + p3[...].reshape(11 * n, 384).astype(F32)
     final = jnp.maximum(final, 0.0).astype(BF)
     line = jnp.concatenate([final[y * n : y * n + n] for y in range(11)], axis=1)
-    out[...] = jnp.maximum(dot(line, ptk[...]), 0.0).astype(BF)
-
-
-def encode(frames, conv_first, conv_second, conv_third, res_first, res_second, projection):
+    return jnp.maximum(dot(line, ptk[...]), 0.0).astype(BF)
+
+
+def step(
+    frames, proj, hidden, cells, w_in, w_rec, w1, w2, w3, r1, r2, counts, ids, reset, bias, head,
+    out, hout, cout, *scratch,
+):
+    raw, enc, (pt, hid, cell, win, wrec, hall), own = scratch[0], scratch[1:17], scratch[17:23], scratch[23:35]
+    sem_q, sem_w, sem_x = scratch[35:]
+    dp, tp = Ring("dp", "tensor"), Ring("tensor", "dp")
+    pairs = raw.shape[0]
+    loads = [
+        pltpu.make_async_copy(src, dst, sem_w.at[i])
+        for i, (src, dst) in enumerate(
+            [(hidden, hid), (proj, pt), (w_rec, wrec), (w_in, win), (cells, cell)]
+        )
+    ]
+
+    def fetch(q):
+        return pltpu.make_async_copy(frames.at[:, q], raw.at[q], sem_q.at[q])
+
+    def start(q, _):
+        fetch(q).start()
+        return 0
+
+    loads[0].start()
+    loads[1].start()
+    lax.fori_loop(0, pairs, start, 0)
+    for load in loads[2:]:
+        load.start()
+    own[4][...] = jnp.zeros_like(own[4])
+    sent = []
+
+    def share_hidden():
+        loads[0].wait()
+        greet((dp, tp))
+        sent.append(send_hidden(tp, ids, reset, hid, hall, sem_x))
+
+    def rest():
+        for load in loads[2:]:
+            load.wait()
+
+    feat = encoder(fetch, loads[1].wait, share_hidden, w1, w2, w3, r1, r2, pt, raw, *enc)
+    core(
+        feat, dp, tp, sent[0], rest, counts, ids, reset, bias, head, hid, cell, win, wrec,
+        out, hout, cout, hall, *own,
+    )
+
+
+def body(
+    frames, counts, slot_ids, reset_flags, hidden_state, cell_state, conv_first, conv_second,
+    conv_third, res_first, res_second, projection, input_weight, recur_weight, gate_bias, head_weight,
+):
     n = frames.shape[0]
+    share, slots = hidden_state.shape
+    nd, nt = lax.axis_size("dp"), lax.axis_size("tensor")
+    rows = slot_ids.shape[1]
+    per = rows // nt
     tiles = frames.transpose(0, 2, 1, 3).reshape(n, 42, 8, 84)
     flatw = lambda w: w.transpose(2, 3, 1, 0).reshape(-1, w.shape[0])
     vm = lambda *s: pltpu.VMEM(s, BF)
     vmf = lambda *s: pltpu.VMEM(s, F32)
+    pairs = lambda m: pltpu.SemaphoreType.DMA((2, m))
+    anywhere = pl.BlockSpec(memory_space=pl.ANY)
+    local = pl.BlockSpec(memory_space=pltpu.VMEM)
+    width = input_weight.shape[2]
     return pl.pallas_call(
-        encoder,
-        out_shape=jax.ShapeDtypeStruct((n, 256), BF),
-        in_specs=[pl.BlockSpec(memory_space=pl.ANY)] + [pl.BlockSpec(memory_space=pltpu.VMEM)] * 6,
-        out_specs=pl.BlockSpec(memory_space=pltpu.VMEM),
+        step,
+        out_shape=[
+            jax.ShapeDtypeStruct((head_weight.shape[0], n), F32),
+            jax.ShapeDtypeStruct((share, slots), F32),
+            jax.ShapeDtypeStruct((share, slots), F32),
+        ],
+        in_specs=[anywhere] * 6 + [local] * 10,
+        out_specs=[local] * 3,
         scratch_shapes=[
-            vm(42, n, 8, 84), vmf(n * 8, 128), vm(512, 768), vm(384, 256), vm(768, 256),
+            vm(42, n, 8, 84),
+            vmf(n * 8, 128), vm(512, 768), vm(384, 256), vm(768, 256),
             vm(1152, 256), vm(1152, 384), vm(1152, 384), vmf(2, 3872, 128), vm(4224, 256),
             vm(87, n, 768), vmf(6 * n, 256), vm(45, n, 896), vm(24, n, 896),
-            vm(11, n, 384), vm(13, n, 384), vm(13, n, 384), pltpu.SemaphoreType.DMA((42,)),
+            vm(11, n, 384), vm(13, n, 384), vm(13, n, 384),
+            vm(3872, 256), vmf(share, slots), vmf(share, slots), vm(4 * share, width),
+            vm(4 * share, nt * share), vm(nt, share, rows),
+            vmf(nd, 1, width), vmf(nd, 1, width), vm(nt, per, width), vmf(nt, per, 128),
+            vmf(nt, per, 128), vmf(nd, 1, 128), vmf(nd, 1, 128), vmf(4 * share, rows),
+            pairs(nd), pairs(nt), pairs(nt), pairs(nd),
+            pltpu.SemaphoreType.DMA((42,)), pltpu.SemaphoreType.DMA((5,)), pairs(nt),
         ],
-        compiler_params=pltpu.CompilerParams(vmem_limit_bytes=60 * 1024 * 1024),
-    )(tiles, flatw(conv_first), flatw(conv_second), flatw(conv_third), flatw(res_first), flatw(res_second), projection.T)
-
-
-def joined_along(blocks, dim):
-    lengths = list(blocks.shape[1:])
-    lengths[dim] *= blocks.shape[0]
-    return jnp.moveaxis(blocks, 0, dim).reshape(lengths)
-
-
-def gather_together(arrays, axis, dims):
-    ravelled = jnp.concatenate([a.reshape(-1) for a in arrays])
-    lines, at, outs = (lax.all_gather(ravelled, axis), 0, [])
-    for a, dim in zip(arrays, dims):
-        blocks = lines[:, at : at + a.size].reshape(-1, *a.shape)
-        outs.append(joined_along(blocks, dim))
-        at += a.size
-    return tuple(outs)
-
-
-def copy_for_each(shard, axis):
-    copies = jnp.broadcast_to(shard, (lax.axis_size(axis), *shard.shape))
-    return lax.all_to_all(copies, axis, split_axis=0, concat_axis=0, tiled=True)
-
-
-def over_copies(shard, axis):
-    everything = copy_for_each(shard, axis)
-    return jnp.sum(everything, axis=0)
-
-
-def body(
-    frames,
-    counts,
-    slot_ids,
-    reset_flags,
-    hidden_state,
-    cell_state,
-    conv_first,
-    conv_second,
-    conv_third,
-    res_first,
-    res_second,
-    projection,
-    input_weight,
-    recur_weight,
-    gate_bias,
-    head_weight,
-):
-    dp_count = lax.axis_size("dp")
-    tensor_count = lax.axis_size("tensor")
-    dp_index = lax.axis_index("dp")
-    tensor_index = lax.axis_index("tensor")
-    capacity = frames.shape[0]
-    pair_depth = capacity // dp_count
-    per_device = slot_ids.shape[1] // tensor_count
-    tallies = lax.dynamic_index_in_dim(counts, tensor_index, 0, keepdims=False)
-    starts = jnp.cumsum(tallies, dtype=jnp.int32) - tallies
-    range_ends = starts + tallies
-    own_start = lax.dynamic_index_in_dim(starts, dp_index, 0, keepdims=False)
-    own_count = lax.dynamic_index_in_dim(tallies, dp_index, 0, keepdims=False)
-    peer_index = jnp.arange(dp_count, dtype=jnp.int32)
-    levels = jnp.arange(pair_depth, dtype=jnp.int32)
-    send_rows = ((peer_index[:, None] - own_start) % dp_count + levels[None, :] * dp_count).reshape(
-        -1
+        compiler_params=pltpu.CompilerParams(
+            vmem_limit_bytes=60 * 1024 * 1024, collective_id=0, has_side_effects=True
+        ),
+    )(
+        tiles, projection.T, hidden_state, cell_state, input_weight.reshape(4 * share, width),
+        recur_weight.reshape(4 * share, nt * share), flatw(conv_first), flatw(conv_second),
+        flatw(conv_third), flatw(res_first), flatw(res_second), counts, slot_ids, reset_flags,
+        gate_bias, jnp.pad(head_weight, ((0, 13), (0, 0))),
     )
-    send_live = send_rows < own_count
-    send_safe = jnp.minimum(send_rows, capacity - 1)
-    balanced_ranks = jnp.arange(per_device, dtype=jnp.int32) * dp_count + dp_index
-    source = jnp.sum((range_ends[:, None] <= balanced_ranks[None, :]).astype(jnp.int32), axis=0)
-    offset = balanced_ranks - jnp.take(starts, source)
-    take_slots = source * pair_depth + offset // dp_count
-    own = encode(
-        frames, conv_first, conv_second, conv_third, res_first, res_second, projection
-    )
-    outgoing = jnp.where(
-        send_live[:, None], jnp.take(own, send_safe, axis=0), jnp.zeros((), jnp.bfloat16)
-    )
-    incoming = lax.all_to_all(outgoing, "dp", split_axis=0, concat_axis=0, tiled=True)
-    features = jnp.take(incoming, take_slots, axis=0).T
-    chosen = slot_ids[0]
-    keep_state = (1 - jnp.take(reset_flags[0], chosen)).astype(jnp.float32)
-    prev_hidden = jnp.take(hidden_state, chosen, axis=1) * keep_state[None, :]
-    prev_cell = jnp.take(cell_state, chosen, axis=1) * keep_state[None, :]
-    all_features, all_hidden = gather_together(
-        (features, prev_hidden.astype(jnp.bfloat16)), "tensor", (1, 0)
-    )
-    hidden_share = hidden_state.shape[0]
-    gate_sums = jnp.dot(
-        input_weight.reshape(4 * hidden_share, -1), all_features, preferred_element_type=jnp.float32
-    )
-    gate_sums = gate_sums + jnp.dot(
-        recur_weight.reshape(4 * hidden_share, -1), all_hidden, preferred_element_type=jnp.float32
-    )
-    gate_sums = (gate_sums + gate_bias.reshape(4 * hidden_share, 1)).reshape(4, hidden_share, -1)
-    next_cell = jax.nn.sigmoid(gate_sums[1]) * prev_cell + jax.nn.sigmoid(gate_sums[0]) * jnp.tanh(
-        gate_sums[2]
-    )
-    next_hidden = jax.nn.sigmoid(gate_sums[3]) * jnp.tanh(next_cell)
-    hidden_after = hidden_state.at[:, chosen].set(next_hidden)
-    cell_after = cell_state.at[:, chosen].set(next_cell)
-    partial_heads = jnp.dot(
-        head_weight, next_hidden.astype(jnp.bfloat16), preferred_element_type=jnp.float32
-    )
-    totals = over_copies(partial_heads, "tensor")
-    own_heads = lax.dynamic_slice_in_dim(totals, tensor_index * per_device, per_device, 1)
-    back_rows = (dp_index - starts[:, None]) % dp_count + levels[None, :] * dp_count
-    back_live = (back_rows < tallies[:, None]).reshape(-1)
-    back_place = jnp.minimum((starts[:, None] + back_rows) // dp_count, per_device - 1).reshape(-1)
-    outgoing_heads = jnp.where(back_live[None, :], jnp.take(own_heads, back_place, axis=1), 0.0)
-    returned = lax.all_to_all(outgoing_heads, "dp", split_axis=1, concat_axis=1, tiled=True)
-    arrivals = jnp.arange(capacity, dtype=jnp.int32)
-    home_slots = (own_start + arrivals) % dp_count * pair_depth + arrivals // dp_count
-    policy_out = jnp.where(
-        (arrivals < own_count)[None, :], jnp.take(returned, home_slots, axis=1), 0.0
-    )
-    return (policy_out, hidden_after, cell_after)
 
 
 def solution(mesh):

time: 141 us -> 88.9 us (0.63)
  Pallas kernels: 43.6 us -> 75.7 us
  starting transfers between devices: 27.1 us -> 0 us
  blocking collectives: 23.1 us -> 0 us
  local copies, waits for them, and re-layouts: 22.6 us -> 12.1 us
  waiting for transfers between devices: 10.4 us -> 0 us
  other arithmetic: 8.79 us -> 0 us
  matrix products: 4.21 us -> 0 us
    pallas_call x1, Pallas kernels: 43.6 us -> 75.7 us  [body(): pl.pallas_call(step, out_shape=[jax.ShapeDtypeStruct((head_weight.shape[0...]
    all_to_all x3 -> x0, starting transfers between devices: 27.1 us -> none  [the longest x1 13.4 us: body(): lax.all_to_all(outgoing_heads, 'dp', split_axis=1, concat_axis=1, tiled=T...]
    all_gather x1 -> x0, blocking collectives: 23.1 us -> none  [gather_together(): lines, at, outs = (lax.all_gather(ravelled, axis), 0, [])]
    all_to_all x3 -> x0, waiting for transfers between devices: 10.4 us -> none  [the longest x1 7.56 us: copy_for_each(): return lax.all_to_all(copies, axis, split_axis=0, concat_axis=0, tiled=True)]
    gather x8 -> x0, local copies, waits for them, and re-layouts: 6.49 us -> none  [the longest x1 1.32 us: body(): jnp.take(own, send_safe, axis=0)]
    dot_general x3 -> x0, matrix products: 4.21 us -> none  [the longest x1 3.71 us: body(): jnp.dot(recur_weight.reshape(4 * hidden_share, -1), all_hidden, preferred...]
    and x5 -> x0, other arithmetic: 3.27 us -> none  [the longest x1 1.26 us: body(): jnp.take(returned, home_slots, axis=1)]
    select_n x12 -> x0, other arithmetic: 3.08 us -> none  [the longest x2 0.73 us: body(): jnp.where(send_live[:, None], jnp.take(own, send_safe, axis=0), jnp.zeros...]
  transfers between devices with their start and end apart: 3 -> 0, of which waited for: 3 -> 0; matrix products, arithmetic and copies ran while one was open for 8% -> 0% of each run, Pallas kernels for 0% -> 0%
where the time goes in v1:
time: 88.9 us; the launch traced here: 88.5 us
  Pallas kernels  75.7 us (85%)
  local copies, waits for them, and re-layouts  12.1 us (14%)
    pallas_call x1, Pallas kernels, body(): pl.pallas_call(step, out_shape=[jax.ShapeDtypeStruct((head_weight.shape[0...  75.7 us
    transpose x3, local copies, waits for them, and re-layouts, body(): flatw = lambda w: w.transpose(2, 3, 1, 0).reshape(-1, w.shape[0])  4.84 us
    unnamed x3, local copies, waits for them, and re-layouts  4.64 us

profile of v1, /device:TPU:1, one launch (start us, length us, event | category | flops | bytes accessed | tf_op | source)
XLA Modules:
  0.0 88.5 jit_solution(5161643992122657790)
XLA Ops:
  0.6 1.3 %reshape.33.w1 = bf16[36,16]{1,0:T(8,128)(2,1)} reshape(bf16[3,3,4,16]{3,2,1,0:T(4,128)(2,1)} %bitcast.27) | data formatting | bytes 2304 | tf_op jit(solution)/shard_map/reshape | solution.py:423
  1.9 1.3 %pad.4.head = bf16[32,256]{1,0:T(8,128)(2,1)} pad(bf16[19,256]{1,0:T(8,128)(2,1)} %param.31, bf16[]{:T(256)} %constant.2.clone.1), padding=0_13x0_0 | pad | bytes 26114 | tf_op jit(solution)/shard_map/jit(_pad)/pad | solution.py:459
  3.3 1.6 %copy.22 = bf16[3,3,32,32]{3,2,1,0:T(8,128)(2,1)} copy(bf16[3,3,32,32]{2,3,1,0:T(8,128)(2,1)} %bitcast.23) | data formatting | bytes 36864 | tf_op jit(solution)/shard_map/transpose | solution.py:423
  4.9 1.6 %copy.23 = bf16[3,3,32,32]{3,2,1,0:T(8,128)(2,1)} copy(bf16[3,3,32,32]{2,3,1,0:T(8,128)(2,1)} %bitcast.24) | data formatting | bytes 36864 | tf_op jit(solution)/shard_map/transpose | solution.py:423
  6.5 1.6 %copy.24 = bf16[3,3,32,32]{3,2,1,0:T(8,128)(2,1)} copy(bf16[3,3,32,32]{2,3,1,0:T(8,128)(2,1)} %bitcast.25) | data formatting | bytes 36864 | tf_op jit(solution)/shard_map/transpose | solution.py:423
  8.1 75.7 %shard_map.175 = (f32[19,32]{1,0:T(8,128)}, f32[256,256]{1,0:T(8,128)}, f32[256,256]{1,0:T(8,128)}) custom-call(bf16[32,42,8,84]{3,2,1,0:T(8,128)(2,1)} %bitcast.17, bf16[3872,256]{1,0:T(8,128)(2,1)} %bitcast.18, f32[256,256]{1,0:T(8,128)} %hidden.1, f32[256,256]{1,0:T(8,128)} %cells.1, bf16[1024,256]{1,0:T(8,128)(2,1)} %bitcast.19, ...), custom_call_target="tpu_custom_call" | custom-call | tf_op jit(solution)/shard_map/pallas_call | solution.py:430
  83.8 1.3 %copy.28 = f32[19,32]{1,0:T(8,128)} copy(f32[19,32]{1,0:T(8,128)} %get-tuple-element.6) | data formatting | bytes 4864
  85.1 1.7 %copy.29 = f32[256,256]{1,0:T(8,128)} copy(f32[256,256]{1,0:T(8,128)} %get-tuple-element.7) | data formatting | bytes 524288
  86.8 1.7 %copy.30 = f32[256,256]{1,0:T(8,128)} copy(f32[256,256]{1,0:T(8,128)} %get-tuple-element.8) | data formatting | bytes 524288

commit v2 on v1

v2 whole, which is shorter than its diff:
```python
import jax
import jax.numpy as jnp
from jax import lax
from jax.experimental import pallas as pl
from jax.experimental.pallas import tpu as pltpu
from jax.sharding import PartitionSpec as P

BF = jnp.bfloat16
F32 = jnp.float32
NEG = -3.0e38


def lanes(shape, dim):
    return lax.broadcasted_iota(jnp.int32, shape, dim)


def dot(a, b):
    return jnp.dot(a, b, preferred_element_type=F32)


def spread(w, width):
    pick = (lanes((width, 128), 1) % width == lanes((width, 128), 0)).astype(BF)
    return dot(w, pick)


def spread_turned(w):
    pick = (lanes((32, 128), 1) % 32 == lanes((32, 128), 0)).astype(BF)
    return jnp.concatenate(
        [
            lax.dot_general(
                w[k * 32 : k * 32 + 32, :], pick, (((0,), (0,)), ((), ())), preferred_element_type=F32
            )
            for k in range(9)
        ],
        axis=0,
    )


def band_weights(out_ref, tiled, depth, spots, per_lane, columns, first):
    width = 128 // per_lane
    lane = lanes((depth, 128), 1) // width
    for ky in range(3):
        for p in range(spots):
            for col in range(columns):
                block = None
                for i in range(per_lane):
                    start = first(col, i)
                    if start is None:
                        continue
                    kx = p - start
                    if 0 <= kx <= 2:
                        row = (ky * 3 + kx) * depth
                        part = jnp.where(lane == i, tiled[row : row + depth], 0.0)
                        block = part if block is None else block + part
                if block is None:
                    block = jnp.zeros((depth, 128), F32)
                row = (ky * spots + p) * depth
                out_ref[row : row + depth, col * 128 : col * 128 + 128] = block.astype(BF)


def column_mask(n, test):
    return jnp.where(test(lanes((n, 128), 1)), 1.0, 0.0).astype(BF)


def shifted(parts, pitch):
    inside = column_mask(parts[0].shape[0], lambda lane: lane < 128 - pitch) > 0.5
    rolled = [pltpu.roll(a, 128 - pitch, 1) for a in parts]
    return [
        jnp.where(inside, rolled[v], rolled[min(v + 1, len(parts) - 1)])
        for v in range(len(parts))
    ]


def alternate(count, produce, consume):
    produce(0, 0)

    def body(i, _):
        produce(2 * i + 1, 1)
        consume(2 * i, 0)
        produce(2 * i + 2, 0)
        consume(2 * i + 1, 1)
        return 0

    lax.fori_loop(0, (count - 1) // 2, body, 0)
    consume(count - 1, 0)


def count_tables(counts, me_t, me_d, cap, per):
    nd = counts.shape[1]
    own = counts[pl.ds(me_t, 1), :].astype(F32)
    a_row = lanes((nd, nd), 1)
    a_col = lanes((nd, nd), 0)
    wide = jnp.broadcast_to(own, (nd, nd))
    start_col = jnp.sum(jnp.where(a_row < a_col, wide, 0.0), axis=1, keepdims=True)
    count_col = jnp.sum(jnp.where(a_row == a_col, wide, 0.0), axis=1, keepdims=True)
    start_row = jnp.sum(
        jnp.where(a_col < a_row, jnp.broadcast_to(count_col, (nd, nd)), 0.0), axis=0, keepdims=True
    )
    mine = lanes((1, nd), 1) == me_d
    start = jnp.sum(jnp.where(mine, start_row, 0.0), axis=1, keepdims=True).astype(jnp.int32)
    count = jnp.sum(jnp.where(mine, own, 0.0), axis=1, keepdims=True).astype(jnp.int32)
    b, j = lanes((nd, cap), 0), lanes((nd, cap), 1)
    send = (jnp.bitwise_and(b - start - j, nd - 1) == 0) & (j < count)
    rank = (lanes((per, nd), 0) * nd + me_d).astype(F32)
    take = (start_row <= rank) & (rank < start_row + own)
    rank = (lanes((nd, per), 1) * nd + me_d).astype(F32)
    give = (start_col <= rank) & (rank < start_col + count_col)
    j, b = lanes((cap, nd), 0), lanes((cap, nd), 1)
    home = (jnp.bitwise_and(b - start - j, nd - 1) == 0) & (j < count)
    as_f32 = lambda m: jnp.where(m, 1.0, 0.0)
    return as_f32(send), as_f32(take), as_f32(give), as_f32(home)


def dot_nt(a, b):
    return lax.dot_general(a, b, (((1,), (1,)), ((), ())), preferred_element_type=F32)


def chosen_rows(a, b, turn=False):
    value, pick = (a, b.astype(BF)) if turn else (b, a.astype(BF))
    high = value.astype(BF)
    rest = value - high.astype(F32)
    middle = rest.astype(BF)
    terms = (high, middle, (rest - middle.astype(F32)).astype(BF))
    parts = [dot(t, pick) if turn else dot(pick, t) for t in terms]
    return parts[0] + parts[1] + parts[2]


class Ring:
    def __init__(self, axis, other):
        self.axis, self.size, self.me = axis, lax.axis_size(axis), lax.axis_index(axis)
        self.other = lax.axis_index(other)

    def place(self, peer):
        return (peer, self.other) if self.axis == "dp" else (self.other, peer)

    def each(self, act):
        def step(i, _):
            k = 1 + lax.rem(i + self.size * 3 // 8, self.size - 1)
            act(k, lax.rem(self.me + k, self.size))
            return 0

        lax.fori_loop(0, self.size - 1, step, 0)

    def copy(self, k, peer, src, dst, sems):
        return pltpu.make_async_remote_copy(
            src_ref=src, dst_ref=dst, send_sem=sems.at[0, k], recv_sem=sems.at[1, k],
            device_id=self.place(peer), device_id_type=pl.DeviceIdType.MESH,
        )


def greet(rings):
    barrier = pltpu.get_barrier_semaphore()
    for ring in rings:
        ring.each(
            lambda k, peer, ring=ring: pl.semaphore_signal(
                barrier, inc=1, device_id=ring.place(peer), device_id_type=pl.DeviceIdType.MESH
            )
        )
    pl.semaphore_wait(barrier, sum(ring.size - 1 for ring in rings))


def send_hidden(ring, ids, reset, hid, hall, sems):
    slots, rows = hid.shape[1], ids.shape[1]
    keep = (1 - reset[...]).astype(F32)
    pick = jnp.where(lanes((slots, rows), 0) == ids[...], 1.0, 0.0)
    hall[ring.me] = dot((hid[...] * keep).astype(BF), pick.astype(BF)).astype(BF)
    copy = lambda k, peer: ring.copy(k, peer, hall.at[ring.me], hall.at[ring.me], sems)
    ring.each(lambda k, peer: copy(k, peer).start())
    return copy


def core(
    feat, dp, tp, hidden_copy, waits, tables, stores,
    ids, reset, bias, head, hid, cell, win, wrec,
    out, hout, cout,
    hall, orow, inrow, fall, hp, hin, brow, rrow, gates, sem_f, sem_g, sem_h, sem_b,
):
    per = fall.shape[1]
    share, slots = hid.shape
    rows = ids.shape[1]
    send, take, give, home = tables

    spread_rows = dot(send.astype(BF), feat)
    for b in range(dp.size):
        orow[b] = spread_rows[b : b + 1]
    inrow[dp.me] = orow[dp.me]
    row_copy = lambda k, peer: dp.copy(k, peer, orow.at[peer], inrow.at[dp.me], sem_f)
    dp.each(lambda k, peer: row_copy(k, peer).start())

    waits()
    keep = (1 - reset[...]).astype(F32)
    pick = jnp.where(lanes((slots, rows), 0) == ids[...], 1.0, 0.0)
    tp.each(lambda k, peer: hidden_copy(k, peer).wait())
    everyone = hall[...].reshape(tp.size * share, rows)
    recurrent = []
    for q in range(4):
        tall = jnp.transpose(jnp.broadcast_to(bias[q : q + 1, :], (8, share)))[:, 0:1]
        gates[q * share : (q + 1) * share] = dot(wrec[q * share : (q + 1) * share], everyone) + tall
    prev_cell = chosen_rows(cell[...] * keep, pick, True)

    dp.each(lambda k, peer: row_copy(k, peer).wait())
    gathered = jnp.concatenate([inrow[a] for a in range(dp.size)], axis=0)
    fall[tp.me] = dot(take.astype(BF), gathered.astype(BF)).astype(BF)
    feat_copy = lambda k, peer: tp.copy(k, peer, fall.at[tp.me], fall.at[tp.me], sem_g)
    tp.each(lambda k, peer: feat_copy(k, peer).start())
    tp.each(lambda k, peer: feat_copy(k, peer).wait())

    features = fall[...].reshape(rows, fall.shape[2])
    sums = gates[...] + dot_nt(win[...], features)
    gate = [sums[q * share : (q + 1) * share] for q in range(4)]
    next_cell = jax.nn.sigmoid(gate[1]) * prev_cell + jax.nn.sigmoid(gate[0]) * jnp.tanh(gate[2])
    next_hidden = jax.nn.sigmoid(gate[3]) * jnp.tanh(next_cell)
    partial = jnp.transpose(dot(head[...], next_hidden.astype(BF)))
    width = partial.shape[1]
    for t in range(tp.size):
        hp[t, :, 0:width] = partial[t * per : (t + 1) * per]
    hin[tp.me] = hp[tp.me]
    sum_copy = lambda k, peer: tp.copy(k, peer, hp.at[peer], hin.at[tp.me], sem_h)
    tp.each(lambda k, peer: sum_copy(k, peer).start())

    square = lanes((rows, rows), 0) == lanes((rows, rows), 1)
    column = jnp.sum(jnp.where(square, ids[...], 0).astype(F32), axis=1, keepdims=True)
    lay = jnp.where(lanes((rows, slots), 1).astype(F32) == column, 1.0, 0.0)
    chosen = jnp.sum(lay, axis=0, keepdims=True) > 0.0
    hout[...] = jnp.where(chosen, chosen_rows(next_hidden, lay, True), hid[...])
    cout[...] = jnp.where(chosen, chosen_rows(next_cell, lay, True), cell[...])

    for store in stores:
        store.start()
    tp.each(lambda k, peer: sum_copy(k, peer).wait())
    total = hin[0]
    for t in range(1, tp.size):
        total = total + hin[t]
    back = chosen_rows(give, total)
    for a in range(dp.size):
        brow[a] = back[a : a + 1]
    rrow[dp.me] = brow[dp.me]
    back_copy = lambda k, peer: dp.copy(k, peer, brow.at[peer], rrow.at[dp.me], sem_b)
    dp.each(lambda k, peer: back_copy(k, peer).start())
    dp.each(lambda k, peer: back_copy(k, peer).wait())
    heads = chosen_rows(home, jnp.concatenate([rrow[a] for a in range(dp.size)], axis=0))
    out[...] = jnp.transpose(heads)[0 : out.shape[0], :]
    for store in stores:
        store.wait()


def encoder(
    fetch, ready, after_weights, w1, w2, w3, r1, r2, pt,
    raw, flat, sel, k1, k2, k3, kr1, kr2, ptf, ptk, u, carry, p1, p2, p3, p3r, q1,
    wide0, wide1, acc0, acc1, third,
):
    pairs, n = raw.shape[0:2]
    wide, acc = (wide0, wide1), (acc0, acc1)
    ready("conv")
    x = lanes((128, 768), 0)
    col = lanes((128, 768), 1)
    p = col % 32
    hit = (x == (col // 128) * 16 - 11 + p) & (p < 18)
    for c in range(4):
        sel[c * 128 : c * 128 + 128] = jnp.where(hit & (col // 32 % 4 == c), 1.0, 0.0).astype(BF)
    t1 = [spread(w1[k // 3, k % 3], 16) for k in range(9)]
    t1 = [jnp.concatenate([t, t], axis=1) for t in t1]
    kx = lanes((32, 256), 0) - 2 * (lanes((32, 256), 1) // 16 % 8) - lanes((32, 256), 1) // 128
    for ky in range(3):
        for c in range(4):
            block = jnp.zeros((32, 256), F32)
            for k in range(3):
                block = jnp.where(kx == k, t1[ky * 3 + k][c : c + 1], block)
            row = ky * 128 + c * 32
            k1[row : row + 32] = block.astype(BF)
    both = lambda col, i: 2 * i + col
    band_weights(k2, spread(w2[...], 32), 16, 16, 4, 2, both)
    band_weights(k3, spread_turned(w3), 32, 12, 4, 2, both)
    same = lambda col, i: None if col * 4 + i > 10 else col * 4 + i - 1
    band_weights(kr1, spread_turned(r1), 32, 12, 4, 3, same)
    band_weights(kr2, spread_turned(r2), 32, 12, 4, 3, same)

    after_weights()
    ready("dense")

    def widen(i, _):
        rows = pl.ds(i * 352, 352)
        block = pt[rows, :].astype(F32)
        ptf[0, rows, :] = block[:, :128]
        ptf[1, rows, :] = block[:, 128:]
        return 0

    lax.fori_loop(0, 11, widen, 0)

    def reorder(y, _):
        for px in range(11):
            rows = pl.ds(y * 384 + px * 32, 32)
            for h in range(2):
                ptk[rows, h * 128 : h * 128 + 128] = ptf[
                    h, pl.ds(y * 11 + px, 32, stride=121), :
                ].astype(BF)
        ptk[pl.ds(y * 384 + 352, 32), :] = jnp.zeros((32, 256), BF)
        return 0

    lax.fori_loop(0, 11, reorder, 0)

    u[0] = jnp.zeros((n, 768), BF)
    u[2 * pairs + 1] = jnp.zeros((n, 768), BF)
    u[2 * pairs + 2] = jnp.zeros((n, 768), BF)
    p1[0] = jnp.zeros((n, 896), BF)
    p1[43] = jnp.zeros((n, 896), BF)
    p1[44] = jnp.zeros((n, 896), BF)
    p2[0] = jnp.zeros((n, 896), BF)
    p2[22] = jnp.zeros((n, 896), BF)
    p2[23] = jnp.zeros((n, 896), BF)
    for ref in (p3r, q1):
        ref[0] = jnp.zeros((n, 384), BF)
        ref[12] = jnp.zeros((n, 384), BF)
    flat[...] = jnp.zeros_like(flat)

    batch = 6

    def unpack(i, slot):
        for g in range(batch):
            q = i * batch + g
            fetch(q).wait()
            flat[slot, g, :, 0:84] = raw[q].astype(F32).reshape(n * 8, 84)
        for g in range(batch):
            for y in range(2):
                for c in range(4):
                    wide[slot][(g * 2 + y) * n : (g * 2 + y + 1) * n, c * 128 : c * 128 + 128] = (
                        flat[slot, g, pl.ds(y * 4 + c, n, stride=8), :].astype(BF)
                    )

    def cut(i, slot):
        got = dot(wide[slot][...], sel[...]).astype(BF)
        u[pl.ds(i * 2 * batch + 1, 2 * batch)] = got.reshape(2 * batch, n, 768)

    alternate(pairs // batch, unpack, cut)

    def conv_row(src, y, count, step, width):
        taps = [src[y + ky] for ky in range(3)]
        return [
            jnp.concatenate([t[:, v * step : v * step + width] for t in taps], axis=1)
            for v in range(count)
        ]

    def conv_rows(src, y, rows, count, step, width, weights):
        lhs = [a for r in range(rows) for a in conv_row(src, y + r, count, step, width)]
        return dot(jnp.concatenate(lhs, axis=0), weights[...]).astype(BF)

    zero = jnp.zeros((), BF)

    def pool_stage(src, dst, group, count, step, width, weights, per, pitch, offset, limit, last):
        size = count * n
        carry[0:size] = conv_rows(src, 0, 1, count, step, width, weights)
        first = column_mask(n, lambda lane: lane // pitch >= offset) > 0.5
        final = column_mask(
            n, lambda lane: lane // pitch + ((count - 1) * per - offset) < limit
        ) > 0.5

        def produce(i, slot):
            acc[slot][0 : 2 * group * size] = conv_rows(
                src, 2 * group * i + 1, 2 * group, count, step, width, weights
            )

        def consume(i, slot):
            for g in range(group):
                y = i * group + g
                row = lambda r, v, h: acc[slot][
                    r * size + v * n : r * size + v * n + n, h * 128 : h * 128 + 128
                ]
                keep = jnp.where(y < last, 1.0, 0.0).astype(BF) if g == group - 1 else None
                half = []
                for h in range(2):
                    tops = []
                    for v in range(count):
                        now, later = row(2 * g, v, h), row(2 * g + 1, v, h)
                        if keep is not None:
                            later = later * keep
                        if g == 0:
                            before = carry[v * n : v * n + n, h * 128 : h * 128 + 128]
                        else:
                            before = row(2 * g - 1, v, h)
                        tops.append(jnp.maximum(jnp.maximum(before, now), jnp.maximum(later, zero)))
                        if g == group - 1:
                            carry[v * n : v * n + n, h * 128 : h * 128 + 128] = later
                    half.append(tops)
                even, odd = half
                even[-1] = jnp.where(final, even[-1], zero)
                nxt = shifted(even, pitch)
                for v in range(count):
                    best = jnp.maximum(jnp.maximum(even[v], odd[v]), nxt[v])
                    if v == 0:
                        best = jnp.where(first, best, zero)
                    if v == count - 1:
                        best = jnp.where(final, best, zero)
                    dst[y + 1, :, v * 128 : v * 128 + 128] = best
                dst[y + 1, :, count * 128 : count * 128 + 128] = jnp.zeros((n, 128), BF)

        alternate((last + 1) // group, produce, consume)

    pool_stage(u, p1, 2, 6, 128, 128, k1, 8, 16, 5, 42, 41)
    pool_stage(p1, p2, 1, 6, 128, 256, k2, 4, 32, 2, 21, 20)

    for y in range(0, 21, 7):
        third[y * 3 * n : (y + 7) * 3 * n] = conv_rows(p2, y, 7, 3, 256, 384, k3)
    low = jnp.full((), NEG, BF)
    begin = column_mask(n, lambda lane: lane >= 32) > 0.5
    inner = column_mask(n, lambda lane: lane < 96) > 0.5
    for y in range(11):
        half = []
        for h in range(2):
            tops = []
            for v in range(3):
                top = None
                for r in range(max(2 * y - 1, 0), min(2 * y + 2, 21)):
                    at = (r * 3 + v) * n
                    part = third[at : at + n, h * 128 : h * 128 + 128]
                    top = part if top is None else jnp.maximum(top, part)
                tops.append(top)
            half.append(tops)
        even, odd = half
        even[0] = jnp.where(begin, even[0], low)
        even[2] = jnp.where(inner, even[2], low)
        nxt = shifted(even, 32)
        for v in range(3):
            best = jnp.maximum(jnp.maximum(even[v], odd[v]), nxt[v])
            if v == 2:
                best = jnp.where(inner, best, zero)
            p3[y, :, v * 128 : v * 128 + 128] = best
            p3r[y + 1, :, v * 128 : v * 128 + 128] = jnp.maximum(best, zero)

    def full_rows(src):
        return jnp.concatenate(
            [jnp.concatenate([src[y + ky] for ky in range(3)], axis=1) for y in range(11)], axis=0
        )

    q1[1:12] = jnp.maximum(dot(full_rows(p3r), kr1[...]), 0.0).astype(BF).reshape(11, n, 384)
    final = dot(full_rows(q1), kr2[...]) + p3[...].reshape(11 * n, 384).astype(F32)
    final = jnp.maximum(final, 0.0).astype(BF)
    line = jnp.concatenate([final[y * n : y * n + n] for y in range(11)], axis=1)
    return jnp.maximum(dot(line, ptk[...]), 0.0).astype(BF)


def step(*refs):
    hbm, (out, hout, cout) = refs[:16], refs[16:19]
    held, (raw, *enc), own = refs[19:34], refs[34:34 + 22], refs[34 + 22:46 + 22]
    hnew, cnew, hall, sem_q, sem_w, sem_x, sem_o = refs[46 + 22:]
    dp, tp = Ring("dp", "tensor"), Ring("tensor", "dp")
    frames = hbm[0]
    loads = [pltpu.make_async_copy(hbm[i + 1], held[i], sem_w.at[i]) for i in range(15)]
    names = ("pt", "hid", "cell", "win", "wrec", "w1", "w2", "w3", "r1", "r2")
    at = {name: i for i, name in enumerate(names + ("counts", "ids", "reset", "bias", "head"))}
    ref = lambda *which: [held[at[name]] for name in which]
    groups = {
        "conv": ("w1", "w2", "w3", "r1", "r2"),
        "dense": ("pt",),
        "hidden": ("hid", "counts", "ids", "reset"),
        "rest": ("cell", "win", "wrec", "bias", "head"),
    }

    def ready(group):
        for name in groups[group]:
            loads[at[name]].wait()

    def fetch(q):
        return pltpu.make_async_copy(frames.at[:, q], raw.at[q], sem_q.at[q])

    def start(q, _):
        fetch(q).start()
        return 0

    for name in groups["conv"] + groups["hidden"]:
        loads[at[name]].start()
    lax.fori_loop(0, raw.shape[0], start, 0)
    for name in groups["dense"] + groups["rest"]:
        loads[at[name]].start()
    own[4][...] = jnp.zeros_like(own[4])
    sent = []
    counts, ids, reset, hid = ref("counts", "ids", "reset", "hid")

    def share_hidden():
        ready("hidden")
        sent.extend(count_tables(counts, tp.me, dp.me, frames.shape[0], own[2].shape[1]))
        greet((dp, tp))
        sent.append(send_hidden(tp, ids, reset, hid, hall, sem_x))

    feat = encoder(fetch, ready, share_hidden, *ref(*groups["conv"], "pt"), raw, *enc)
    stores = [
        pltpu.make_async_copy(hnew, hout, sem_o.at[0]),
        pltpu.make_async_copy(cnew, cout, sem_o.at[1]),
    ]
    core(
        feat, dp, tp, sent[4], lambda: ready("rest"), sent[0:4], stores, ids, reset,
        *ref("bias", "head", "hid", "cell", "win", "wrec"), out, hnew, cnew, hall, *own,
    )


def hand_over(*refs):
    for i in range(3):
        refs[3 + i][...] = refs[i][...]


def body(
    frames, counts, slot_ids, reset_flags, hidden_state, cell_state, conv_first, conv_second,
    conv_third, res_first, res_second, projection, input_weight, recur_weight, gate_bias, head_weight,
):
    n = frames.shape[0]
    share, slots = hidden_state.shape
    nd, nt = lax.axis_size("dp"), lax.axis_size("tensor")
    rows = slot_ids.shape[1]
    per = rows // nt
    width = input_weight.shape[2]
    vm = lambda *s: pltpu.VMEM(s, BF)
    vmf = lambda *s: pltpu.VMEM(s, F32)
    pairs = lambda m: pltpu.SemaphoreType.DMA((2, m))
    anywhere = pl.BlockSpec(memory_space=pl.ANY)
    local = pl.BlockSpec(memory_space=pltpu.VMEM)
    turned = lambda w: w.transpose(2, 3, 0, 1).reshape(-1, w.shape[1])
    operands = [
        frames.transpose(0, 2, 1, 3).reshape(n, 42, 8, 84),
        projection.T, hidden_state, cell_state, input_weight.reshape(4 * share, width),
        recur_weight.reshape(4 * share, nt * share), conv_first.transpose(2, 3, 1, 0),
        conv_second.transpose(2, 3, 1, 0).reshape(144, 32), turned(conv_third), turned(res_first),
        turned(res_second), counts, slot_ids, reset_flags, gate_bias, head_weight,
    ]
    shapes = [
        jax.ShapeDtypeStruct((head_weight.shape[0], n), F32),
        jax.ShapeDtypeStruct((share, slots), F32),
        jax.ShapeDtypeStruct((share, slots), F32),
    ]
    results = pl.pallas_call(
        step,
        out_shape=shapes,
        in_specs=[anywhere] * 16,
        out_specs=[local, anywhere, anywhere],
        scratch_shapes=[pltpu.VMEM(a.shape, a.dtype) for a in operands[1:]] + [
            vm(42, n, 8, 84),
            vmf(2, 6, n * 8, 128), vm(512, 768), vm(384, 256), vm(768, 256),
            vm(1152, 256), vm(1152, 384), vm(1152, 384), vmf(2, 3872, 128), vm(4224, 256),
            vm(87, n, 768), vm(6 * n, 256), vm(45, n, 896), vm(24, n, 896),
            vm(11, n, 384), vm(13, n, 384), vm(13, n, 384),
            vm(12 * n, 512), vm(12 * n, 512), vm(24 * n, 256), vm(24 * n, 256), vm(63 * n, 256),
            vmf(nd, 1, width), vmf(nd, 1, width), vm(nt, per, width), vmf(nt, per, 128),
            vmf(nt, per, 128), vmf(nd, 1, 128), vmf(nd, 1, 128), vmf(4 * share, rows),
            pairs(nd), pairs(nt), pairs(nt), pairs(nd),
            vmf(share, slots), vmf(share, slots), vm(nt, share, rows),
            pltpu.SemaphoreType.DMA((42,)), pltpu.SemaphoreType.DMA((15,)), pairs(nt),
            pltpu.SemaphoreType.DMA((2,)),
        ],
        compiler_params=pltpu.CompilerParams(
            vmem_limit_bytes=60 * 1024 * 1024, collective_id=0, has_side_effects=True
        ),
    )(*operands)
    return pl.pallas_call(
        hand_over, out_shape=shapes, in_specs=[local] * 3, out_specs=[local] * 3
    )(*results)


def solution(mesh):
    return jax.shard_map(
        body,
        mesh=mesh,
        in_specs=(
            P(("dp", "tensor"), None, None, None),
            P(),
            P("dp", None),
            P("dp", None),
            P("tensor", "dp"),
            P("tensor", "dp"),
            P(),
            P(),
            P(),
            P(),
            P(),
            P(),
            P(None, "tensor", None),
            P(None, "tensor", None),
            P(None, "tensor"),
            P(None, "tensor"),
        ),
        out_specs=(P(None, ("dp", "tensor")), P("tensor", "dp"), P("tensor", "dp")),
        check_vma=False,
    )
```

time: 88.9 us -> 62.6 us (0.70)
  Pallas kernels: 75.7 us -> 61.8 us
  local copies, waits for them, and re-layouts: 12.1 us -> 0 us
    pallas_call x1 -> x2, Pallas kernels: 75.7 us -> 61.8 us  [the longest x1 59.9 us: body(): pl.pallas_call(step, out_shape=shapes, in_specs=[anywhere] * 16, out_spec...]
    transpose x3 -> x0, local copies, waits for them, and re-layouts: 4.84 us -> none  [body(): flatw = lambda w: w.transpose(2, 3, 1, 0).reshape(-1, w.shape[0])]
    unnamed x3 -> x0, local copies, waits for them, and re-layouts: 4.64 us -> none
    reshape x1 -> x0, local copies, waits for them, and re-layouts: 1.32 us -> none  [body(): flatw = lambda w: w.transpose(2, 3, 1, 0).reshape(-1, w.shape[0])]
    pad x1 -> x0, local copies, waits for them, and re-layouts: 1.31 us -> none  [body(): jnp.pad(head_weight, ((0, 13), (0, 0)))]
where the time goes in v2:
time: 62.6 us; the launch traced here: 62.4 us
  Pallas kernels  61.8 us (99%)
  between operations  0.65 us (1%)
    pallas_call x1, Pallas kernels, body(): pl.pallas_call(step, out_shape=shapes, in_specs=[anywhere] * 16, out_spec...  59.9 us
    pallas_call x1, Pallas kernels, body(): pl.pallas_call(hand_over, out_shape=shapes, in_specs=[local] * 3, out_spe...  1.86 us

profile of v2, /device:TPU:1, one launch (start us, length us, event | category | flops | bytes accessed | tf_op | source)
XLA Modules:
  0.0 62.4 jit_solution(1306860789883188318)
XLA Ops:
  0.6 59.9 %shard_map.175 = (f32[19,32]{1,0:T(8,128)}, f32[256,256]{1,0:T(8,128)}, f32[256,256]{1,0:T(8,128)}) custom-call(bf16[32,42,8,84]{3,2,1,0:T(8,128)(2,1)} %bitcast.20, bf16[3872,256]{1,0:T(8,128)(2,1)} %bitcast.21, f32[256,256]{1,0:T(8,128)} %refs_2_.1, f32[256,256]{1,0:T(8,128)} %refs_3_.1, bf16[1024,256]{1,0:T(8,128)(2,1)} %bitcast.22, ...), custom_call_target="tpu_custom_call" | custom-call | tf_op jit(solution)/shard_map/pallas_call | solution.py:528
  60.6 1.9 %shard_map.176 = (f32[19,32]{1,0:T(8,128)}, f32[256,256]{1,0:T(8,128)}, f32[256,256]{1,0:T(8,128)}) custom-call(f32[19,32]{1,0:T(8,128)} %get-tuple-element.6.refs_0_, f32[256,256]{1,0:T(8,128)} %get-tuple-element.7.refs_1_, f32[256,256]{1,0:T(8,128)} %get-tuple-element.8.refs_2_), custom_call_target="tpu_custom_call" | custom-call | tf_op jit(solution)/shard_map/pallas_call | solution.py:551

commit v3 on v2

--- a/solution.py
+++ b/solution.py
@@ -136,10 +136,10 @@
     def each(self, act):
         def step(i, _):
             k = 1 + lax.rem(i + self.size * 3 // 8, self.size - 1)
-            act(k, lax.rem(self.me + k, self.size))
+            act(k, jnp.bitwise_and(self.me + k, self.size - 1))
             return 0
 
-        lax.fori_loop(0, self.size - 1, step, 0)
+        lax.fori_loop(0, self.size - 1, step, 0, unroll=True)
 
     def copy(self, k, peer, src, dst, sems):
         return pltpu.make_async_remote_copy(
@@ -156,7 +156,10 @@
                 barrier, inc=1, device_id=ring.place(peer), device_id_type=pl.DeviceIdType.MESH
             )
         )
-    pl.semaphore_wait(barrier, sum(ring.size - 1 for ring in rings))
+
+
+def meet(rings):
+    pl.semaphore_wait(pltpu.get_barrier_semaphore(), sum(ring.size - 1 for ring in rings))
 
 
 def send_hidden(ring, ids, reset, hid, hall, sems):
@@ -245,29 +248,36 @@
 
 
 def encoder(
-    fetch, ready, after_weights, w1, w2, w3, r1, r2, pt,
+    fetch, ready, after_cut, w1, w2, w3, r1, r2, pt,
     raw, flat, sel, k1, k2, k3, kr1, kr2, ptf, ptk, u, carry, p1, p2, p3, p3r, q1,
     wide0, wide1, acc0, acc1, third,
 ):
     pairs, n = raw.shape[0:2]
     wide, acc = (wide0, wide1), (acc0, acc1)
     ready("conv")
-    x = lanes((128, 768), 0)
-    col = lanes((128, 768), 1)
-    p = col % 32
-    hit = (x == (col // 128) * 16 - 11 + p) & (p < 18)
-    for c in range(4):
-        sel[c * 128 : c * 128 + 128] = jnp.where(hit & (col // 32 % 4 == c), 1.0, 0.0).astype(BF)
+    column = lanes((256, 384), 1)
+    window, spot = column // 64, column % 64
+    source = spot // 18 * 128 + window * 16 - 11 + spot % 18
+    x = lanes((256, 384), 0)
+    inside = (spot < 36) & (source // 128 == spot // 18) & (source >= 0)
+    sel[...] = jnp.where(inside & (source == x), 1.0, 0.0).astype(BF)
     t1 = [spread(w1[k // 3, k % 3], 16) for k in range(9)]
     t1 = [jnp.concatenate([t, t], axis=1) for t in t1]
-    kx = lanes((32, 256), 0) - 2 * (lanes((32, 256), 1) // 16 % 8) - lanes((32, 256), 1) // 128
-    for ky in range(3):
-        for c in range(4):
-            block = jnp.zeros((32, 256), F32)
-            for k in range(3):
-                block = jnp.where(kx == k, t1[ky * 3 + k][c : c + 1], block)
-            row = ky * 128 + c * 32
-            k1[row : row + 32] = block.astype(BF)
+    row = lanes((128, 256), 0)
+    spot = row % 40
+    kx = spot % 18 - 2 * (lanes((128, 256), 1) // 16 % 8) - lanes((128, 256), 1) // 128
+    code = jnp.where((kx >= 0) & (kx <= 2) & (spot < 36), row // 40 * 6 + spot // 18 * 3 + kx, -1)
+    for pair in range(2):
+        block = jnp.zeros((128, 256), F32)
+        for ky in range(3):
+            for c in range(2):
+                for k in range(3):
+                    line = t1[ky * 3 + k][pair * 2 + c : pair * 2 + c + 1]
+                    block = jnp.where(code == ky * 6 + c * 3 + k, line, block)
+        block = block.astype(BF)
+        k1[0, pair * 128 : pair * 128 + 128] = block
+        k1[1, pair * 128 : pair * 128 + 64] = block[64:]
+        k1[1, pair * 128 + 64 : pair * 128 + 128] = block[:64]
     both = lambda col, i: 2 * i + col
     band_weights(k2, spread(w2[...], 32), 16, 16, 4, 2, both)
     band_weights(k3, spread_turned(w3), 32, 12, 4, 2, both)
@@ -275,7 +285,6 @@
     band_weights(kr1, spread_turned(r1), 32, 12, 4, 3, same)
     band_weights(kr2, spread_turned(r2), 32, 12, 4, 3, same)
 
-    after_weights()
     ready("dense")
 
     def widen(i, _):
@@ -299,9 +308,9 @@
 
     lax.fori_loop(0, 11, reorder, 0)
 
-    u[0] = jnp.zeros((n, 768), BF)
-    u[2 * pairs + 1] = jnp.zeros((n, 768), BF)
-    u[2 * pairs + 2] = jnp.zeros((n, 768), BF)
+    for r in range(3):
+        for y in (0, 2 * pairs + 1, 2 * pairs + 2):
+            u[r, y] = jnp.zeros((2, n, 384), BF)
     p1[0] = jnp.zeros((n, 896), BF)
     p1[43] = jnp.zeros((n, 896), BF)
     p1[44] = jnp.zeros((n, 896), BF)
@@ -323,15 +332,52 @@
         for g in range(batch):
             for y in range(2):
                 for c in range(4):
-                    wide[slot][(g * 2 + y) * n : (g * 2 + y + 1) * n, c * 128 : c * 128 + 128] = (
-                        flat[slot, g, pl.ds(y * 4 + c, n, stride=8), :].astype(BF)
-                    )
+                    line = ((c // 2 * batch + g) * 2 + y) * n
+                    wide[slot][line : line + n, c % 2 * 128 : c % 2 * 128 + 128] = flat[
+                        slot, g, pl.ds(y * 4 + c, n, stride=8), :
+                    ].astype(BF)
 
     def cut(i, slot):
         got = dot(wide[slot][...], sel[...]).astype(BF)
-        u[pl.ds(i * 2 * batch + 1, 2 * batch)] = got.reshape(2 * batch, n, 768)
+        size = 2 * batch * n
+        for pair in range(2):
+            for v in range(3):
+                part = got[pair * size : pair * size + size, v * 128 : v * 128 + 128]
+                for r in range(3):
+                    moved = pltpu.roll(part, 40 * r, 1) if r else part
+                    u[r, pl.ds(i * 2 * batch + 1, 2 * batch), pair, :, v * 128 : v * 128 + 128] = (
+                        moved.reshape(2 * batch, n, 128)
+                    )
 
     alternate(pairs // batch, unpack, cut)
+    after_cut()
+
+    lane_in = lambda a, b: column_mask(n, lambda lane: (lane >= a) & (lane < b)) > 0.5
+    ranges = (
+        (lane_in(0, 40), lane_in(40, 80)),
+        (lane_in(64, 104), column_mask(n, lambda lane: (lane >= 104) | (lane < 16)) > 0.5),
+    )
+
+    def first_conv(target, y, rows):
+        lhs = ([], [])
+        for r in range(rows):
+            for v in range(3):
+                packed = ([], [])
+                for pair in range(2):
+                    a, b, c = (
+                        u[ky, y + r + ky, pair, :, v * 128 : v * 128 + 128] for ky in range(3)
+                    )
+                    for odd in range(2):
+                        at_a, at_b = ranges[odd]
+                        packed[odd].append(jnp.where(at_a, a, jnp.where(at_b, b, c)))
+                for odd in range(2):
+                    lhs[odd].append(jnp.concatenate(packed[odd], axis=1))
+        for odd in range(2):
+            got = dot(jnp.concatenate(lhs[odd], axis=0), k1[odd]).astype(BF)
+            for r in range(rows):
+                for v in range(3):
+                    line = (r * 6 + 2 * v + odd) * n
+                    target[line : line + n] = got[(r * 3 + v) * n : (r * 3 + v + 1) * n]
 
     def conv_row(src, y, count, step, width):
         taps = [src[y + ky] for ky in range(3)]
@@ -346,18 +392,19 @@
 
     zero = jnp.zeros((), BF)
 
-    def pool_stage(src, dst, group, count, step, width, weights, per, pitch, offset, limit, last):
+    def second_conv(target, y, rows):
+        target[0 : rows * 6 * n] = conv_rows(p1, y, rows, 6, 128, 256, k2)
+
+    def pool_stage(conv, dst, group, count, per, pitch, offset, limit, last):
         size = count * n
-        carry[0:size] = conv_rows(src, 0, 1, count, step, width, weights)
+        conv(carry, 0, 1)
         first = column_mask(n, lambda lane: lane // pitch >= offset) > 0.5
         final = column_mask(
             n, lambda lane: lane // pitch + ((count - 1) * per - offset) < limit
         ) > 0.5
 
         def produce(i, slot):
-            acc[slot][0 : 2 * group * size] = conv_rows(
-                src, 2 * group * i + 1, 2 * group, count, step, width, weights
-            )
+            conv(acc[slot], 2 * group * i + 1, 2 * group)
 
         def consume(i, slot):
             for g in range(group):
@@ -395,8 +442,8 @@
 
         alternate((last + 1) // group, produce, consume)
 
-    pool_stage(u, p1, 2, 6, 128, 128, k1, 8, 16, 5, 42, 41)
-    pool_stage(p1, p2, 1, 6, 128, 256, k2, 4, 32, 2, 21, 20)
+    pool_stage(first_conv, p1, 2, 6, 8, 16, 5, 42, 41)
+    pool_stage(second_conv, p2, 1, 6, 4, 32, 2, 21, 20)
 
     for y in range(0, 21, 7):
         third[y * 3 * n : (y + 7) * 3 * n] = conv_rows(p2, y, 7, 3, 256, 384, k3)
@@ -466,6 +513,7 @@
         fetch(q).start()
         return 0
 
+    greet((dp, tp))
     for name in groups["conv"] + groups["hidden"]:
         loads[at[name]].start()
     lax.fori_loop(0, raw.shape[0], start, 0)
@@ -478,7 +526,7 @@
     def share_hidden():
         ready("hidden")
         sent.extend(count_tables(counts, tp.me, dp.me, frames.shape[0], own[2].shape[1]))
-        greet((dp, tp))
+        meet((dp, tp))
         sent.append(send_hidden(tp, ids, reset, hid, hall, sem_x))
 
     feat = encoder(fetch, ready, share_hidden, *ref(*groups["conv"], "pt"), raw, *enc)
@@ -493,8 +541,24 @@
 
 
 def hand_over(*refs):
-    for i in range(3):
-        refs[3 + i][...] = refs[i][...]
+    given, results, held, sems = refs[0:3], refs[3:6], refs[6:9], refs[9]
+    half = held[1].shape[0] // 2
+    spans = [(0, pl.ds(0, held[0].shape[0]))]
+    spans += [(i, pl.ds(k * half, half)) for k in range(2) for i in (1, 2)]
+    moves = [
+        [
+            pltpu.make_async_copy(src[i].at[rows], dst[i].at[rows], sems.at[way, at])
+            for way, (src, dst) in enumerate(((given, held), (held, results)))
+        ]
+        for at, (i, rows) in enumerate(spans)
+    ]
+    for inward, _ in moves:
+        inward.start()
+    for inward, outward in moves:
+        inward.wait()
+        outward.start()
+    for _, outward in moves:
+        outward.wait()
 
 
 def body(
@@ -532,11 +596,11 @@
         out_specs=[local, anywhere, anywhere],
         scratch_shapes=[pltpu.VMEM(a.shape, a.dtype) for a in operands[1:]] + [
             vm(42, n, 8, 84),
-            vmf(2, 6, n * 8, 128), vm(512, 768), vm(384, 256), vm(768, 256),
+            vmf(2, 6, n * 8, 128), vm(256, 384), vm(2, 256, 256), vm(768, 256),
             vm(1152, 256), vm(1152, 384), vm(1152, 384), vmf(2, 3872, 128), vm(4224, 256),
-            vm(87, n, 768), vm(6 * n, 256), vm(45, n, 896), vm(24, n, 896),
+            vm(3, 87, 2, n, 384), vm(6 * n, 256), vm(45, n, 896), vm(24, n, 896),
             vm(11, n, 384), vm(13, n, 384), vm(13, n, 384),
-            vm(12 * n, 512), vm(12 * n, 512), vm(24 * n, 256), vm(24 * n, 256), vm(63 * n, 256),
+            vm(24 * n, 256), vm(24 * n, 256), vm(24 * n, 256), vm(24 * n, 256), vm(63 * n, 256),
             vmf(nd, 1, width), vmf(nd, 1, width), vm(nt, per, width), vmf(nt, per, 128),
             vmf(nt, per, 128), vmf(nd, 1, 128), vmf(nd, 1, 128), vmf(4 * share, rows),
             pairs(nd), pairs(nt), pairs(nt), pairs(nd),
@@ -549,7 +613,12 @@
         ),
     )(*operands)
     return pl.pallas_call(
-        hand_over, out_shape=shapes, in_specs=[local] * 3, out_specs=[local] * 3
+        hand_over,
+        out_shape=shapes,
+        in_specs=[anywhere] * 3,
+        out_specs=[anywhere] * 3,
+        scratch_shapes=[pltpu.VMEM(a.shape, a.dtype) for a in shapes]
+        + [pltpu.SemaphoreType.DMA((2, 5))],
     )(*results)
 
 

time: 62.6 us -> 55.9 us (0.89)
  Pallas kernels: 61.8 us -> 55 us
    pallas_call x1, Pallas kernels: 59.9 us -> 53.1 us  [body(): pl.pallas_call(step, out_shape=shapes, in_specs=[anywhere] * 16, out_spec...]
where the time goes in v3:
time: 55.9 us; the launch traced here: 55.6 us
  Pallas kernels  55 us (98%)
  between operations  0.65 us (1%)
    pallas_call x1, Pallas kernels, body(): pl.pallas_call(step, out_shape=shapes, in_specs=[anywhere] * 16, out_spec...  53.1 us
    pallas_call x1, Pallas kernels, body(): pl.pallas_call(hand_over, out_shape=shapes, in_specs=[anywhere] * 3, out_...  1.85 us

profile of v3, /device:TPU:1, one launch (start us, length us, event | category | flops | bytes accessed | tf_op | source)
XLA Modules:
  0.0 55.6 jit_solution(2253878916760609280)
XLA Ops:
  0.6 53.1 %shard_map.175 = (f32[19,32]{1,0:T(8,128)}, f32[256,256]{1,0:T(8,128)}, f32[256,256]{1,0:T(8,128)}) custom-call(bf16[32,42,8,84]{3,2,1,0:T(8,128)(2,1)} %bitcast.20, bf16[3872,256]{1,0:T(8,128)(2,1)} %bitcast.21, f32[256,256]{1,0:T(8,128)} %refs_2_.1, f32[256,256]{1,0:T(8,128)} %refs_3_.1, bf16[1024,256]{1,0:T(8,128)(2,1)} %bitcast.22, ...), custom_call_target="tpu_custom_call" | custom-call | tf_op jit(solution)/shard_map/pallas_call | solution.py:592
  53.8 1.9 %shard_map.176 = (f32[19,32]{1,0:T(8,128)}, f32[256,256]{1,0:T(8,128)}, f32[256,256]{1,0:T(8,128)}) custom-call(f32[19,32]{1,0:T(8,128)} %get-tuple-element.6.refs_0_, f32[256,256]{1,0:T(8,128)} %get-tuple-element.7.refs_1_, f32[256,256]{1,0:T(8,128)} %get-tuple-element.8.refs_2_), custom_call_target="tpu_custom_call" | custom-call | tf_op jit(solution)/shard_map/pallas_call | solution.py:615

commit v4 on v3

--- a/solution.py
+++ b/solution.py
@@ -36,7 +36,7 @@
     )
 
 
-def band_weights(out_ref, tiled, depth, spots, per_lane, columns, first):
+def band_weights(out_ref, tiled, depth, spots, per_lane, columns, first, place=None):
     width = 128 // per_lane
     lane = lanes((depth, 128), 1) // width
     for ky in range(3):
@@ -54,7 +54,7 @@
                         block = part if block is None else block + part
                 if block is None:
                     block = jnp.zeros((depth, 128), F32)
-                row = (ky * spots + p) * depth
+                row = (ky * spots + p) * depth if place is None else place(ky, p)
                 out_ref[row : row + depth, col * 128 : col * 128 + 128] = block.astype(BF)
 
 
@@ -143,9 +143,15 @@
 
     def copy(self, k, peer, src, dst, sems):
         return pltpu.make_async_remote_copy(
-            src_ref=src, dst_ref=dst, send_sem=sems.at[0, k], recv_sem=sems.at[1, k],
+            src_ref=src, dst_ref=dst, send_sem=sems.at[0], recv_sem=sems.at[1],
             device_id=self.place(peer), device_id_type=pl.DeviceIdType.MESH,
         )
+
+
+    def finish(self, ref, sems):
+        others = ref.at[pl.ds(0, self.size - 1)]
+        for way in range(2):
+            pltpu.make_async_copy(others, others, sems.at[way]).wait()
 
 
 def greet(rings):
@@ -169,11 +175,10 @@
     hall[ring.me] = dot((hid[...] * keep).astype(BF), pick.astype(BF)).astype(BF)
     copy = lambda k, peer: ring.copy(k, peer, hall.at[ring.me], hall.at[ring.me], sems)
     ring.each(lambda k, peer: copy(k, peer).start())
-    return copy
 
 
 def core(
-    feat, dp, tp, hidden_copy, waits, tables, stores,
+    feat, dp, tp, hidden_sems, waits, tables, stores,
     ids, reset, bias, head, hid, cell, win, wrec,
     out, hout, cout,
     hall, orow, inrow, fall, hp, hin, brow, rrow, gates, sem_f, sem_g, sem_h, sem_b,
@@ -193,7 +198,7 @@
     waits()
     keep = (1 - reset[...]).astype(F32)
     pick = jnp.where(lanes((slots, rows), 0) == ids[...], 1.0, 0.0)
-    tp.each(lambda k, peer: hidden_copy(k, peer).wait())
+    tp.finish(hall, hidden_sems)
     everyone = hall[...].reshape(tp.size * share, rows)
     recurrent = []
     for q in range(4):
@@ -201,12 +206,12 @@
         gates[q * share : (q + 1) * share] = dot(wrec[q * share : (q + 1) * share], everyone) + tall
     prev_cell = chosen_rows(cell[...] * keep, pick, True)
 
-    dp.each(lambda k, peer: row_copy(k, peer).wait())
+    dp.finish(inrow, sem_f)
     gathered = jnp.concatenate([inrow[a] for a in range(dp.size)], axis=0)
     fall[tp.me] = dot(take.astype(BF), gathered.astype(BF)).astype(BF)
     feat_copy = lambda k, peer: tp.copy(k, peer, fall.at[tp.me], fall.at[tp.me], sem_g)
     tp.each(lambda k, peer: feat_copy(k, peer).start())
-    tp.each(lambda k, peer: feat_copy(k, peer).wait())
+    tp.finish(fall, sem_g)
 
     features = fall[...].reshape(rows, fall.shape[2])
     sums = gates[...] + dot_nt(win[...], features)
@@ -230,7 +235,7 @@
 
     for store in stores:
         store.start()
-    tp.each(lambda k, peer: sum_copy(k, peer).wait())
+    tp.finish(hin, sem_h)
     total = hin[0]
     for t in range(1, tp.size):
         total = total + hin[t]
@@ -240,7 +245,7 @@
     rrow[dp.me] = brow[dp.me]
     back_copy = lambda k, peer: dp.copy(k, peer, brow.at[peer], rrow.at[dp.me], sem_b)
     dp.each(lambda k, peer: back_copy(k, peer).start())
-    dp.each(lambda k, peer: back_copy(k, peer).wait())
+    dp.finish(rrow, sem_b)
     heads = chosen_rows(home, jnp.concatenate([rrow[a] for a in range(dp.size)], axis=0))
     out[...] = jnp.transpose(heads)[0 : out.shape[0], :]
     for store in stores:
@@ -279,7 +284,9 @@
         k1[1, pair * 128 : pair * 128 + 64] = block[64:]
         k1[1, pair * 128 + 64 : pair * 128 + 128] = block[:64]
     both = lambda col, i: 2 * i + col
-    band_weights(k2, spread(w2[...], 32), 16, 16, 4, 2, both)
+    tail = lambda ky, p: ky * 128 + p * 16 if p < 8 else 384 + ky * 32 + (p - 8) * 16
+    band_weights(k2, spread(w2[...], 32), 16, 10, 4, 2, both, tail)
+    k2[480:512] = jnp.zeros((32, 256), BF)
     band_weights(k3, spread_turned(w3), 32, 12, 4, 2, both)
     same = lambda col, i: None if col * 4 + i > 10 else col * 4 + i - 1
     band_weights(kr1, spread_turned(r1), 32, 12, 4, 3, same)
@@ -311,12 +318,12 @@
     for r in range(3):
         for y in (0, 2 * pairs + 1, 2 * pairs + 2):
             u[r, y] = jnp.zeros((2, n, 384), BF)
-    p1[0] = jnp.zeros((n, 896), BF)
-    p1[43] = jnp.zeros((n, 896), BF)
-    p1[44] = jnp.zeros((n, 896), BF)
-    p2[0] = jnp.zeros((n, 896), BF)
-    p2[22] = jnp.zeros((n, 896), BF)
-    p2[23] = jnp.zeros((n, 896), BF)
+    for r in range(3):
+        for y in (0, 43, 44):
+            p1[r, y] = jnp.zeros((n, 896), BF)
+    p2[0, 0] = jnp.zeros((n, 896), BF)
+    p2[0, 22] = jnp.zeros((n, 896), BF)
+    p2[0, 23] = jnp.zeros((n, 896), BF)
     for ref in (p3r, q1):
         ref[0] = jnp.zeros((n, 384), BF)
         ref[12] = jnp.zeros((n, 384), BF)
@@ -392,10 +399,20 @@
 
     zero = jnp.zeros((), BF)
 
+    end_a, end_b = lane_in(0, 32), lane_in(32, 64)
+
     def second_conv(target, y, rows):
-        target[0 : rows * 6 * n] = conv_rows(p1, y, rows, 6, 128, 256, k2)
-
-    def pool_stage(conv, dst, group, count, per, pitch, offset, limit, last):
+        lhs = []
+        for r in range(rows):
+            for v in range(6):
+                here, after = v * 128, v * 128 + 128
+                main = [p1[0, y + r + ky, :, here : here + 128] for ky in range(3)]
+                a, b, c = (p1[ky, y + r + ky, :, after : after + 128] for ky in range(3))
+                ends = jnp.where(end_a, a, jnp.where(end_b, b, c))
+                lhs.append(jnp.concatenate(main + [ends], axis=1))
+        target[0 : rows * 6 * n] = dot(jnp.concatenate(lhs, axis=0), k2[...]).astype(BF)
+
+    def pool_stage(conv, dst, group, count, per, pitch, offset, limit, last, copies):
         size = count * n
         conv(carry, 0, 1)
         first = column_mask(n, lambda lane: lane // pitch >= offset) > 0.5
@@ -437,16 +454,19 @@
                         best = jnp.where(first, best, zero)
                     if v == count - 1:
                         best = jnp.where(final, best, zero)
-                    dst[y + 1, :, v * 128 : v * 128 + 128] = best
-                dst[y + 1, :, count * 128 : count * 128 + 128] = jnp.zeros((n, 128), BF)
+                    for r in range(copies):
+                        moved = pltpu.roll(best, 32 * r, 1) if r else best
+                        dst[r, y + 1, :, v * 128 : v * 128 + 128] = moved
+                for r in range(copies):
+                    dst[r, y + 1, :, count * 128 : count * 128 + 128] = jnp.zeros((n, 128), BF)
 
         alternate((last + 1) // group, produce, consume)
 
-    pool_stage(first_conv, p1, 2, 6, 8, 16, 5, 42, 41)
-    pool_stage(second_conv, p2, 1, 6, 4, 32, 2, 21, 20)
+    pool_stage(first_conv, p1, 6, 6, 8, 16, 5, 42, 41, 3)
+    pool_stage(second_conv, p2, 3, 6, 4, 32, 2, 21, 20, 1)
 
     for y in range(0, 21, 7):
-        third[y * 3 * n : (y + 7) * 3 * n] = conv_rows(p2, y, 7, 3, 256, 384, k3)
+        third[y * 3 * n : (y + 7) * 3 * n] = conv_rows(p2.at[0], y, 7, 3, 256, 384, k3)
     low = jnp.full((), NEG, BF)
     begin = column_mask(n, lambda lane: lane >= 32) > 0.5
     inner = column_mask(n, lambda lane: lane < 96) > 0.5
@@ -527,7 +547,7 @@
         ready("hidden")
         sent.extend(count_tables(counts, tp.me, dp.me, frames.shape[0], own[2].shape[1]))
         meet((dp, tp))
-        sent.append(send_hidden(tp, ids, reset, hid, hall, sem_x))
+        send_hidden(tp, ids, reset, hid, hall, sem_x)
 
     feat = encoder(fetch, ready, share_hidden, *ref(*groups["conv"], "pt"), raw, *enc)
     stores = [
@@ -535,7 +555,7 @@
         pltpu.make_async_copy(cnew, cout, sem_o.at[1]),
     ]
     core(
-        feat, dp, tp, sent[4], lambda: ready("rest"), sent[0:4], stores, ids, reset,
+        feat, dp, tp, sem_x, lambda: ready("rest"), sent[0:4], stores, ids, reset,
         *ref("bias", "head", "hid", "cell", "win", "wrec"), out, hnew, cnew, hall, *own,
     )
 
@@ -573,7 +593,7 @@
     width = input_weight.shape[2]
     vm = lambda *s: pltpu.VMEM(s, BF)
     vmf = lambda *s: pltpu.VMEM(s, F32)
-    pairs = lambda m: pltpu.SemaphoreType.DMA((2, m))
+    pair = pltpu.SemaphoreType.DMA((2,))
     anywhere = pl.BlockSpec(memory_space=pl.ANY)
     local = pl.BlockSpec(memory_space=pltpu.VMEM)
     turned = lambda w: w.transpose(2, 3, 0, 1).reshape(-1, w.shape[1])
@@ -596,17 +616,16 @@
         out_specs=[local, anywhere, anywhere],
         scratch_shapes=[pltpu.VMEM(a.shape, a.dtype) for a in operands[1:]] + [
             vm(42, n, 8, 84),
-            vmf(2, 6, n * 8, 128), vm(256, 384), vm(2, 256, 256), vm(768, 256),
+            vmf(2, 6, n * 8, 128), vm(256, 384), vm(2, 256, 256), vm(512, 256),
             vm(1152, 256), vm(1152, 384), vm(1152, 384), vmf(2, 3872, 128), vm(4224, 256),
-            vm(3, 87, 2, n, 384), vm(6 * n, 256), vm(45, n, 896), vm(24, n, 896),
+            vm(3, 87, 2, n, 384), vm(6 * n, 256), vm(3, 45, n, 896), vm(1, 24, n, 896),
             vm(11, n, 384), vm(13, n, 384), vm(13, n, 384),
-            vm(24 * n, 256), vm(24 * n, 256), vm(24 * n, 256), vm(24 * n, 256), vm(63 * n, 256),
+            vm(24 * n, 256), vm(24 * n, 256), vm(72 * n, 256), vm(72 * n, 256), vm(63 * n, 256),
             vmf(nd, 1, width), vmf(nd, 1, width), vm(nt, per, width), vmf(nt, per, 128),
             vmf(nt, per, 128), vmf(nd, 1, 128), vmf(nd, 1, 128), vmf(4 * share, rows),
-            pairs(nd), pairs(nt), pairs(nt), pairs(nd),
+            pair, pair, pair, pair,
             vmf(share, slots), vmf(share, slots), vm(nt, share, rows),
-            pltpu.SemaphoreType.DMA((42,)), pltpu.SemaphoreType.DMA((15,)), pairs(nt),
-            pltpu.SemaphoreType.DMA((2,)),
+            pltpu.SemaphoreType.DMA((42,)), pltpu.SemaphoreType.DMA((15,)), pair, pair,
         ],
         compiler_params=pltpu.CompilerParams(
             vmem_limit_bytes=60 * 1024 * 1024, collective_id=0, has_side_effects=True

time: 55.9 us -> 52.3 us (0.936)
  Pallas kernels: 55 us -> 51.4 us
    pallas_call x1, Pallas kernels: 53.1 us -> 49.5 us  [body(): pl.pallas_call(step, out_shape=shapes, in_specs=[anywhere] * 16, out_spec...]
where the time goes in v4:
time: 52.3 us; the launch traced here: 52 us
  Pallas kernels  51.4 us (98%)
  between operations  0.65 us (1%)
    pallas_call x1, Pallas kernels, body(): pl.pallas_call(step, out_shape=shapes, in_specs=[anywhere] * 16, out_spec...  49.5 us
    pallas_call x1, Pallas kernels, body(): pl.pallas_call(hand_over, out_shape=shapes, in_specs=[anywhere] * 3, out_...  1.85 us

profile of v4, /device:TPU:1, one launch (start us, length us, event | category | flops | bytes accessed | tf_op | source)
XLA Modules:
  0.0 52.0 jit_solution(16694149359344463447)
XLA Ops:
  0.6 49.5 %shard_map.175 = (f32[19,32]{1,0:T(8,128)}, f32[256,256]{1,0:T(8,128)}, f32[256,256]{1,0:T(8,128)}) custom-call(bf16[32,42,8,84]{3,2,1,0:T(8,128)(2,1)} %bitcast.20, bf16[3872,256]{1,0:T(8,128)(2,1)} %bitcast.21, f32[256,256]{1,0:T(8,128)} %refs_2_.1, f32[256,256]{1,0:T(8,128)} %refs_3_.1, bf16[1024,256]{1,0:T(8,128)(2,1)} %bitcast.22, ...), custom_call_target="tpu_custom_call" | custom-call | tf_op jit(solution)/shard_map/pallas_call | solution.py:612
  50.2 1.9 %shard_map.176 = (f32[19,32]{1,0:T(8,128)}, f32[256,256]{1,0:T(8,128)}, f32[256,256]{1,0:T(8,128)}) custom-call(f32[19,32]{1,0:T(8,128)} %get-tuple-element.6.refs_0_, f32[256,256]{1,0:T(8,128)} %get-tuple-element.7.refs_1_, f32[256,256]{1,0:T(8,128)} %get-tuple-element.8.refs_2_), custom_call_target="tpu_custom_call" | custom-call | tf_op jit(solution)/shard_map/pallas_call | solution.py:634

commit v5 on v4

--- a/solution.py
+++ b/solution.py
@@ -292,29 +292,6 @@
     band_weights(kr1, spread_turned(r1), 32, 12, 4, 3, same)
     band_weights(kr2, spread_turned(r2), 32, 12, 4, 3, same)
 
-    ready("dense")
-
-    def widen(i, _):
-        rows = pl.ds(i * 352, 352)
-        block = pt[rows, :].astype(F32)
-        ptf[0, rows, :] = block[:, :128]
-        ptf[1, rows, :] = block[:, 128:]
-        return 0
-
-    lax.fori_loop(0, 11, widen, 0)
-
-    def reorder(y, _):
-        for px in range(11):
-            rows = pl.ds(y * 384 + px * 32, 32)
-            for h in range(2):
-                ptk[rows, h * 128 : h * 128 + 128] = ptf[
-                    h, pl.ds(y * 11 + px, 32, stride=121), :
-                ].astype(BF)
-        ptk[pl.ds(y * 384 + 352, 32), :] = jnp.zeros((32, 256), BF)
-        return 0
-
-    lax.fori_loop(0, 11, reorder, 0)
-
     for r in range(3):
         for y in (0, 2 * pairs + 1, 2 * pairs + 2):
             u[r, y] = jnp.zeros((2, n, 384), BF)
@@ -463,6 +440,30 @@
         alternate((last + 1) // group, produce, consume)
 
     pool_stage(first_conv, p1, 6, 6, 8, 16, 5, 42, 41, 3)
+
+    ready("dense")
+
+    def widen(i, _):
+        rows = pl.ds(i * 352, 352)
+        block = pt[rows, :].astype(F32)
+        ptf[0, rows, :] = block[:, :128]
+        ptf[1, rows, :] = block[:, 128:]
+        return 0
+
+    lax.fori_loop(0, 11, widen, 0)
+
+    def reorder(y, _):
+        for px in range(11):
+            rows = pl.ds(y * 384 + px * 32, 32)
+            for h in range(2):
+                ptk[rows, h * 128 : h * 128 + 128] = ptf[
+                    h, pl.ds(y * 11 + px, 32, stride=121), :
+                ].astype(BF)
+        ptk[pl.ds(y * 384 + 352, 32), :] = jnp.zeros((32, 256), BF)
+        return 0
+
+    lax.fori_loop(0, 11, reorder, 0)
+
     pool_stage(second_conv, p2, 3, 6, 4, 32, 2, 21, 20, 1)
 
     for y in range(0, 21, 7):
@@ -533,17 +534,17 @@
         fetch(q).start()
         return 0
 
-    greet((dp, tp))
     for name in groups["conv"] + groups["hidden"]:
         loads[at[name]].start()
     lax.fori_loop(0, raw.shape[0], start, 0)
-    for name in groups["dense"] + groups["rest"]:
-        loads[at[name]].start()
+    greet((dp, tp))
     own[4][...] = jnp.zeros_like(own[4])
     sent = []
     counts, ids, reset, hid = ref("counts", "ids", "reset", "hid")
 
     def share_hidden():
+        for name in groups["dense"] + groups["rest"]:
+            loads[at[name]].start()
         ready("hidden")
         sent.extend(count_tables(counts, tp.me, dp.me, frames.shape[0], own[2].shape[1]))
         meet((dp, tp))

time: 52.3 us -> 51.2 us (0.979)
  Pallas kernels: 51.4 us -> 50.2 us
    pallas_call x1, Pallas kernels: 49.5 us -> 48.3 us  [body(): pl.pallas_call(step, out_shape=shapes, in_specs=[anywhere] * 16, out_spec...]
where the time goes in v5:
time: 51.2 us; the launch traced here: 51 us
  Pallas kernels  50.2 us (98%)
  between operations  0.81 us (2%)
    pallas_call x1, Pallas kernels, body(): pl.pallas_call(step, out_shape=shapes, in_specs=[anywhere] * 16, out_spec...  48.3 us
    pallas_call x1, Pallas kernels, body(): pl.pallas_call(hand_over, out_shape=shapes, in_specs=[anywhere] * 3, out_...  1.85 us

profile of v5, /device:TPU:1, one launch (start us, length us, event | category | flops | bytes accessed | tf_op | source)
XLA Modules:
  0.0 51.0 jit_solution(13517598184636571791)
XLA Ops:
  0.6 48.3 %shard_map.175 = (f32[19,32]{1,0:T(8,128)}, f32[256,256]{1,0:T(8,128)}, f32[256,256]{1,0:T(8,128)}) custom-call(bf16[32,42,8,84]{3,2,1,0:T(8,128)(2,1)} %bitcast.20, bf16[3872,256]{1,0:T(8,128)(2,1)} %bitcast.21, f32[256,256]{1,0:T(8,128)} %refs_2_.1, f32[256,256]{1,0:T(8,128)} %refs_3_.1, bf16[1024,256]{1,0:T(8,128)(2,1)} %bitcast.22, ...), custom_call_target="tpu_custom_call" | custom-call | tf_op jit(solution)/shard_map/pallas_call | solution.py:613
  48.9 1.9 %shard_map.176 = (f32[19,32]{1,0:T(8,128)}, f32[256,256]{1,0:T(8,128)}, f32[256,256]{1,0:T(8,128)}) custom-call(f32[19,32]{1,0:T(8,128)} %get-tuple-element.6.refs_0_, f32[256,256]{1,0:T(8,128)} %get-tuple-element.7.refs_1_, f32[256,256]{1,0:T(8,128)} %get-tuple-element.8.refs_2_), custom_call_target="tpu_custom_call" | custom-call | tf_op jit(solution)/shard_map/pallas_call | solution.py:635
